TPU v7x, 256 devices: a whole 4x4x8 slice. The times are simulated.
256 devices in a mesh: zero: 16 (over z, core), tp: 4 (over x), job: 4 (over y).
Axes of the slice: x: 4, y: 4, z: 8, core: 2. Of those that a mesh axis runs over, the one named last changes fastest.
Arguments:
- w_query: float32 [16384, 4096], P(('job', 'zero'), 'tp'), parts along dimension 0, may hold values from -0.125 to 0.125
- avg_query: float32 [16384, 4096], P(('job', 'zero'), 'tp'), parts along dimension 0, may hold values from -0.09375 to 0.09375
- w_key: float32 [16384, 1024], P(('job', 'zero'), 'tp'), parts along dimension 0, may hold values from -0.125 to 0.125
- avg_key: float32 [16384, 1024], P(('job', 'zero'), 'tp'), parts along dimension 0, may hold values from -0.09375 to 0.09375
- w_value: float32 [16384, 1024], P(('job', 'zero'), 'tp'), parts along dimension 0, may hold values from -0.125 to 0.125
- avg_value: float32 [16384, 1024], P(('job', 'zero'), 'tp'), parts along dimension 0, may hold values from -0.09375 to 0.09375
- norm_train: float32 [16384], P(('job', 'zero', 'tp')), parts along dimension 0, may hold values from 0.25 to 1.75
- norm_step: float32 [16384], P(('job', 'zero', 'tp')), parts along dimension 0, may hold values from -0.3 to 0.3
Outputs:
- serve_query: bfloat16 [16384, 4096], P('job', 'tp'), parts along dimension 0
- serve_key: bfloat16 [16384, 1024], P('job', 'tp'), parts along dimension 0
- serve_value: bfloat16 [16384, 1024], P('job', 'tp'), parts along dimension 0
- column_query: float32 [16384], P(('job', 'tp')), parts along dimension 0
- column_key: float32 [4096], P(('job', 'tp')), parts along dimension 0
- column_value: float32 [4096], P(('job', 'tp')), parts along dimension 0
- serve_norm: bfloat16 [16384], P('job'), parts along dimension 0
- fresh_query: float32 [16384, 4096], P(('job', 'zero'), 'tp'), parts along dimension 0
- fresh_key: float32 [16384, 1024], P(('job', 'zero'), 'tp'), parts along dimension 0
- fresh_value: float32 [16384, 1024], P(('job', 'zero'), 'tp'), parts along dimension 0
There are 4 independent parts, one for each index of `job`. A program takes and returns all parts, laid end to end along the dimension named above; each array names one. Nothing has to cross between parts.
All inputs are finite; a program needn't handle non-finite values.
Results may differ from a plain program's by a relative error of at most 0.001.
Values may be sent and summed in bfloat16 or wider, within the bound.
No kernel may reach another device: no remote copies, remote signals or barrier semaphores. Data moves between devices by JAX's collectives and lax.ppermute only.
A program may use at most 128 MiB of HBM per device.

v0:
```python
import functools

import jax
import jax.numpy as jnp
from jax import lax
from jax.experimental import pallas as pl
from jax.experimental.pallas import tpu as pltpu
from jax.sharding import PartitionSpec as P


keep_rate = 0.75
CHIPS = 8
CORES = 2


def both_ways():
    return [
        (z * CORES + c, (z + 1 - 2 * c) % CHIPS * CORES + c) for z in range(CHIPS) for c in range(CORES)
    ]


def other_core():
    return [(z * CORES + c, z * CORES + 1 - c) for z in range(CHIPS) for c in range(CORES)]


def normalise(everyone, query, key, value, *outs):
    pieces, (column_query, column_key, column_value, gain) = outs[:2], outs[2:]
    wide, narrow = query.shape[1], key.shape[1]
    total = jnp.sum(everyone[...], axis=0, keepdims=True)
    column = jnp.sqrt(total[:, : wide + 2 * narrow])
    column_query[...] = column[:, :wide]
    column_key[...] = column[:, wide : wide + narrow]
    column_value[...] = column[:, wide + narrow :]
    mine = lax.axis_index("tp")
    own = everyone[:, wide + 2 * narrow :]
    size, each = own.shape
    twice = jnp.concatenate([own, own], axis=1).astype(jnp.bfloat16)
    tall = (2 * size, size)
    row, owner = (lax.broadcasted_iota(jnp.int32, tall, d) for d in (0, 1))
    spread = (row == 2 * owner + mine // 2).astype(jnp.bfloat16)
    moved = jnp.dot(spread, twice, preferred_element_type=jnp.float32)
    lane = lax.broadcasted_iota(jnp.int32, moved.shape, 1)
    gain[...] = jnp.where(lane // each == mine % 2, moved, 0.0).astype(gain.dtype)
    rows = pieces[0].shape[0]
    core = lax.axis_index("zero") % CORES
    for piece, half in zip(pieces, (core, 1 - core)):
        at = pl.ds(pl.multiple_of(half * rows, rows), rows)
        piece[:, :wide] = (query[at] / column[:, :wide]).astype(piece.dtype)
        piece[:, wide : wide + narrow] = (key[at] / column[:, wide : wide + narrow]).astype(piece.dtype)
        piece[:, wide + narrow :] = (value[at] / column[:, wide + narrow :]).astype(piece.dtype)


def place(spots, *refs):
    n = len(spots)
    pieces, outs, sems = refs[:n], refs[-4:-1], refs[-1]
    me = lax.axis_index("zero")
    z, c = me // CORES, me % CORES
    copies = []
    for k, (hops, theirs, other) in enumerate(spots):
        rows = pieces[k].shape[0]
        half = 1 - c if theirs else c
        shard = 1 - c if other else c
        chip = (z - hops * (1 - 2 * half) + CHIPS) % CHIPS
        row = pl.multiple_of(((chip * CORES + shard) * 2 + half) * rows, rows)
        column = 0
        for j, out in enumerate(outs):
            wide = out.shape[1]
            copies.append(
                pltpu.make_async_copy(
                    pieces[k].at[:, column : column + wide],
                    out.at[pl.ds(row, rows), :],
                    sems.at[k, j],
                )
            )
            column += wide
    for copy in copies:
        copy.start()
    for copy in copies:
        copy.wait()


def placed(pieces, spots, outs, shapes):
    n = len(pieces)
    before = () if outs is None else tuple(outs)
    size = sum(p.size * 2 for p in pieces)
    pieces = [pltpu.with_memory_space_constraint(p, pltpu.VMEM) for p in pieces]
    return pl.pallas_call(
        functools.partial(place, spots),
        out_shape=shapes,
        in_specs=[pl.BlockSpec(memory_space=pltpu.VMEM)] * n
        + [pl.BlockSpec(memory_space=pl.ANY)] * len(before),
        out_specs=[pl.BlockSpec(memory_space=pl.ANY)] * 3,
        scratch_shapes=[pltpu.SemaphoreType.DMA((n, 3))],
        input_output_aliases={n + j: j for j in range(len(before))},
        cost_estimate=pl.CostEstimate(flops=0, bytes_accessed=2 * size, transcendentals=0),
        compiler_params=pltpu.CompilerParams(vmem_limit_bytes=12 << 20),
        name="place",
    )(*pieces, *before)


def body(w_query, avg_query, w_key, avg_key, w_value, avg_value, norm_train, norm_step):
    fresh_query = keep_rate * avg_query + (1.0 - keep_rate) * w_query
    fresh_key = keep_rate * avg_key + (1.0 - keep_rate) * w_key
    fresh_value = keep_rate * avg_value + (1.0 - keep_rate) * w_value
    depth, wide = fresh_query.shape
    narrow = fresh_key.shape[1]
    gain = (norm_train + norm_step).astype(jnp.bfloat16)
    line = jnp.concatenate(
        [
            jnp.sum(fresh_query * fresh_query, axis=0),
            jnp.sum(fresh_key * fresh_key, axis=0),
            jnp.sum(fresh_value * fresh_value, axis=0),
            gain.astype(jnp.float32),
        ]
    )
    copies = jnp.broadcast_to(line, (CHIPS * CORES, line.size))
    everyone = lax.all_to_all(copies, "zero", split_axis=0, concat_axis=0, tiled=True)

    rows, full = depth // 2, wide + 2 * narrow
    vm = pl.BlockSpec(memory_space=pltpu.VMEM)
    keep, give, column_query, column_key, column_value, gains = pl.pallas_call(
        normalise,
        out_shape=[pltpu.VMEM((rows, full), jnp.bfloat16)] * 2
        + [jax.ShapeDtypeStruct((1, n), jnp.float32) for n in (wide, narrow, narrow)]
        + [pltpu.VMEM((2 * CHIPS * CORES, 2 * gain.size), jnp.bfloat16)],
        in_specs=[vm] * 4,
        out_specs=[vm] * 6,
        compiler_params=pltpu.CompilerParams(vmem_limit_bytes=8 << 20),
        name="normalise",
    )(
        everyone,
        *(pltpu.with_memory_space_constraint(a, pltpu.VMEM) for a in (fresh_query, fresh_key, fresh_value)),
    )

    size = CHIPS * CORES
    def swap(piece):
        return lax.ppermute(piece, "zero", other_core())

    near, far = keep, swap(give)
    held = [
        [
            (keep, (0, False, False)),
            (far, (0, False, True)),
            (swap(keep), (0, True, True)),
            (give, (0, True, False)),
        ]
    ]
    for hop in range(1, CHIPS):
        near = lax.ppermute(near, "zero", both_ways())
        far = lax.ppermute(far, "zero", both_ways())
        held.append(
            [
                (near, (hop, False, False)),
                (far, (hop, False, True)),
                (swap(near), (hop, True, True)),
                (swap(far), (hop, True, False)),
            ]
        )

    shapes = [jax.ShapeDtypeStruct((depth * size, n), jnp.bfloat16) for n in (wide, narrow, narrow)]
    outs = None
    for some in held:
        for two in (some[::2], some[1::2]):
            outs = placed([p for p, _ in two], [s for _, s in two], outs, shapes)
    serve_query, serve_key, serve_value = outs

    tp = lax.axis_size("tp")
    serve_norm = gains
    for k in range(1, tp):
        theirs = lax.ppermute(gains, "tp", [(i, (i + k) % tp) for i in range(tp)])
        serve_norm += theirs
    serve_norm = serve_norm.reshape(-1)
    return (
        serve_query,
        serve_key,
        serve_value,
        column_query.reshape(-1),
        column_key.reshape(-1),
        column_value.reshape(-1),
        serve_norm,
        fresh_query,
        fresh_key,
        fresh_value,
    )


def solution(mesh):
    in_specs = (
        P(("job", "zero"), "tp"),
        P(("job", "zero"), "tp"),
        P(("job", "zero"), "tp"),
        P(("job", "zero"), "tp"),
        P(("job", "zero"), "tp"),
        P(("job", "zero"), "tp"),
        P(("job", "zero", "tp")),
        P(("job", "zero", "tp")),
    )
    out_specs = (
        P("job", "tp"),
        P("job", "tp"),
        P("job", "tp"),
        P(("job", "tp")),
        P(("job", "tp")),
        P(("job", "tp")),
        P("job"),
        P(("job", "zero"), "tp"),
        P(("job", "zero"), "tp"),
        P(("job", "zero"), "tp"),
    )
    return jax.shard_map(body, mesh=mesh, in_specs=in_specs, out_specs=out_specs, check_vma=False)
```

profile of v0, /device:TPU:1, one launch (start us, length us, event | category | flops | bytes accessed | tf_op | source)
XLA Modules:
  0.0 109.9 jit_solution(6980436601083549604)
XLA Ops:
  0.7 1.8 %multiply_reduce_fusion = (f32[1024]{0:T(1024)S(1)}, f32[256,1024]{1,0:T(8,128)S(1)}) fusion(f32[256,1024]{1,0:T(8,128)} %param.8, f32[256,1024]{1,0:T(8,128)} %param.9), kind=kLoop, calls=%fused_computation | loop fusion | flops 1309696 | bytes 3149824 | tf_op jit(solution)/shard_map/reduce_sum | solution.py:110
  2.6 0.0 copy-start
  2.6 0.1 multiply_reduce_fusion.1
  2.8 0.1 broadcast_in_dim.3
  2.8 18.4 %all_to_all.8 = f32[16,1,1600]{2,1,0:T(1,128)S(1)} all-to-all(f32[16,1,1600]{2,1,0:T(1,128)S(1)} %broadcast_in_dim.3), channel_id=1, replica_groups=mesh['zero'=16,'tp'=4,'job'=4] {'zero'}, dimensions={0} | all-to-all | bytes 204800 | tf_op jit(solution)/shard_map/all_to_all | solution.py:117
  21.2 0.6 normalise.1
  21.9 1.7 %collective-permute-done.refs_0_ = bf16[128,1536]{1,0:T(8,128)(2,1)S(1)} collective-permute-done((bf16[128,1536]{1,0:T(8,128)(2,1)S(1)}, bf16[128,1536]{1,0:T(8,128)(2,1)S(1)}, u32[]{:S(2)}, u32[]{:S(2)}) %collective-permute-start) | collective-permute-done | bytes 393248 | tf_op jit(solution)/shard_map/ppermute | solution.py:137
  23.6 5.2 %collective-permute-done.9.refs_0_ = bf16[128,1536]{1,0:T(8,128)(2,1)S(1)} collective-permute-done((bf16[128,1536]{1,0:T(8,128)(2,1)S(1)}, bf16[128,1536]{1,0:T(8,128)(2,1)S(1)}, u32[]{:S(2)}, u32[]{:S(2)}) %collective-permute-start.9) | collective-permute-done | bytes 393248 | tf_op jit(solution)/shard_map/ppermute | solution.py:149
  28.8 0.9 collective-permute-start.10
  29.7 3.3 %collective-permute-done.1.refs_0_ = bf16[128,1536]{1,0:T(8,128)(2,1)S(1)} collective-permute-done((bf16[128,1536]{1,0:T(8,128)(2,1)S(1)}, bf16[128,1536]{1,0:T(8,128)(2,1)S(1)}, u32[]{:S(2)}, u32[]{:S(2)}) %collective-permute-start.1) | collective-permute-done | bytes 393248 | tf_op jit(solution)/shard_map/ppermute | solution.py:150
  33.0 0.9 collective-permute-start.2
  33.9 3.3 %collective-permute-done.10.refs_0_ = bf16[128,1536]{1,0:T(8,128)(2,1)S(1)} collective-permute-done((bf16[128,1536]{1,0:T(8,128)(2,1)S(1)}, bf16[128,1536]{1,0:T(8,128)(2,1)S(1)}, u32[]{:S(2)}, u32[]{:S(2)}) %collective-permute-start.10) | collective-permute-done | bytes 393248 | tf_op jit(solution)/shard_map/ppermute | solution.py:149
  37.2 0.9 collective-permute-start.11
  38.1 3.3 %collective-permute-done.2.refs_0_ = bf16[128,1536]{1,0:T(8,128)(2,1)S(1)} collective-permute-done((bf16[128,1536]{1,0:T(8,128)(2,1)S(1)}, bf16[128,1536]{1,0:T(8,128)(2,1)S(1)}, u32[]{:S(2)}, u32[]{:S(2)}) %collective-permute-start.2) | collective-permute-done | bytes 393248 | tf_op jit(solution)/shard_map/ppermute | solution.py:150
  41.4 0.9 collective-permute-start.3
  42.4 2.2 %collective-permute-start.29 = (bf16[128,1536]{1,0:T(8,128)(2,1)S(1)}, bf16[128,1536]{1,0:T(8,128)(2,1)S(1)}, u32[]{:S(2)}, u32[]{:S(2)}) collective-permute-start(bf16[128,1536]{1,0:T(8,128)(2,1)S(1)} %get-tuple-element.65.refs_0_), channel_id=1, source_target_pairs={{0,16},{16,0},{32,48},{48,32},{64,80},{80,64},{96,112},{112,96},{1... | collective-permute-start | bytes 1179656 | tf_op jit(solution)/shard_map/ppermute | solution.py:137
  44.6 1.1 collective-permute-done.11.refs_0_
  45.7 1.9 %collective-permute-start.12 = (bf16[128,1536]{1,0:T(8,128)(2,1)S(1)}, bf16[128,1536]{1,0:T(8,128)(2,1)S(1)}, u32[]{:S(2)}, u32[]{:S(2)}) collective-permute-start(bf16[128,1536]{1,0:T(8,128)(2,1)S(1)} %collective-permute-done.11.refs_0_), channel_id=1, source_target_pairs={{0,32},{16,240},{32,64},{48,16},{64,96},{80,48},{96,128},{112,80},... | collective-permute-start | bytes 1179656 | tf_op jit(solution)/shard_map/ppermute | solution.py:149
  47.5 2.3 %collective-permute-done.3.refs_0_ = bf16[128,1536]{1,0:T(8,128)(2,1)S(1)} collective-permute-done((bf16[128,1536]{1,0:T(8,128)(2,1)S(1)}, bf16[128,1536]{1,0:T(8,128)(2,1)S(1)}, u32[]{:S(2)}, u32[]{:S(2)}) %collective-permute-start.3) | collective-permute-done | bytes 393248 | tf_op jit(solution)/shard_map/ppermute | solution.py:150
  49.9 0.9 collective-permute-start.4
  50.8 1.2 %collective-permute-start.30 = (bf16[32,128]{1,0:T(8,128)(2,1)S(1)}, bf16[32,128]{1,0:T(8,128)(2,1)S(1)}, u32[]{:S(2)}, u32[]{:S(2)}) collective-permute-start(bf16[32,128]{1,0:T(8,128)(2,1)S(1)} %get-tuple-element.117), channel_id=1, source_target_pairs={{0,4},{4,8},{8,12},{12,0},{1,5},{5,9},{9,13},{13,1},{2,6},{6,10},{... | collective-permute-start | bytes 24584 | tf_op jit(solution)/shard_map/ppermute | solution.py:170
  52.0 2.5 %collective-permute-start.31 = (bf16[32,128]{1,0:T(8,128)(2,1)S(1)}, bf16[32,128]{1,0:T(8,128)(2,1)S(1)}, u32[]{:S(2)}, u32[]{:S(2)}) collective-permute-start(bf16[32,128]{1,0:T(8,128)(2,1)S(1)} %get-tuple-element.117), channel_id=1, source_target_pairs={{0,8},{4,12},{8,0},{12,4},{1,9},{5,13},{9,1},{13,5},{2,10},{6,14},... | collective-permute-start | bytes 24584 | tf_op jit(solution)/shard_map/ppermute | solution.py:170
  54.5 0.3 collective-permute-done.30
  54.8 1.0 collective-permute-start.32
  55.8 0.2 collective-permute-done.31
  56.0 4.2 %collective-permute-start.28 = (bf16[128,1536]{1,0:T(8,128)(2,1)S(1)}, bf16[128,1536]{1,0:T(8,128)(2,1)S(1)}, u32[]{:S(2)}, u32[]{:S(2)}) collective-permute-start(bf16[128,1536]{1,0:T(8,128)(2,1)S(1)} %collective-permute-done.9.refs_0_), channel_id=1, source_target_pairs={{0,16},{16,0},{32,48},{48,32},{64,80},{80,64},{96,112},{112,96},{1... | collective-permute-start | bytes 1179656 | tf_op jit(solution)/shard_map/ppermute | solution.py:137
  60.2 1.9 %collective-permute-start.27 = (bf16[128,1536]{1,0:T(8,128)(2,1)S(1)}, bf16[128,1536]{1,0:T(8,128)(2,1)S(1)}, u32[]{:S(2)}, u32[]{:S(2)}) collective-permute-start(bf16[128,1536]{1,0:T(8,128)(2,1)S(1)} %collective-permute-done.1.refs_0_), channel_id=1, source_target_pairs={{0,16},{16,0},{32,48},{48,32},{64,80},{80,64},{96,112},{112,96},{1... | collective-permute-start | bytes 1179656 | tf_op jit(solution)/shard_map/ppermute | solution.py:137
  62.1 3.2 %collective-permute-start.13 = (bf16[128,1536]{1,0:T(8,128)(2,1)S(1)}, bf16[128,1536]{1,0:T(8,128)(2,1)S(1)}, u32[]{:S(2)}, u32[]{:S(2)}) collective-permute-start(bf16[128,1536]{1,0:T(8,128)(2,1)S(1)} %collective-permute-done.12.refs_0_), channel_id=1, source_target_pairs={{0,32},{16,240},{32,64},{48,16},{64,96},{80,48},{96,128},{112,80},... | collective-permute-start | bytes 1179656 | tf_op jit(solution)/shard_map/ppermute | solution.py:149
  65.3 0.1 collective-permute-start.5
  65.4 0.5 collective-permute-start.24
  65.9 0.1 collective-permute-start.23
  66.0 4.0 %collective-permute-done.13.refs_0_ = bf16[128,1536]{1,0:T(8,128)(2,1)S(1)} collective-permute-done((bf16[128,1536]{1,0:T(8,128)(2,1)S(1)}, bf16[128,1536]{1,0:T(8,128)(2,1)S(1)}, u32[]{:S(2)}, u32[]{:S(2)}) %collective-permute-start.13) | collective-permute-done | bytes 393248 | tf_op jit(solution)/shard_map/ppermute | solution.py:149
  70.0 3.1 %collective-permute-start.14 = (bf16[128,1536]{1,0:T(8,128)(2,1)S(1)}, bf16[128,1536]{1,0:T(8,128)(2,1)S(1)}, u32[]{:S(2)}, u32[]{:S(2)}) collective-permute-start(bf16[128,1536]{1,0:T(8,128)(2,1)S(1)} %collective-permute-done.13.refs_0_), channel_id=1, source_target_pairs={{0,32},{16,240},{32,64},{48,16},{64,96},{80,48},{96,128},{112,80},... | collective-permute-start | bytes 1179656 | tf_op jit(solution)/shard_map/ppermute | solution.py:149
  73.1 1.1 collective-permute-done.5.refs_0_
  74.2 3.1 %collective-permute-start.6 = (bf16[128,1536]{1,0:T(8,128)(2,1)S(1)}, bf16[128,1536]{1,0:T(8,128)(2,1)S(1)}, u32[]{:S(2)}, u32[]{:S(2)}) collective-permute-start(bf16[128,1536]{1,0:T(8,128)(2,1)S(1)} %collective-permute-done.5.refs_0_), channel_id=1, source_target_pairs={{0,32},{16,240},{32,64},{48,16},{64,96},{80,48},{96,128},{112,80},... | collective-permute-start | bytes 1179656 | tf_op jit(solution)/shard_map/ppermute | solution.py:150
  77.4 0.5 collective-permute-start.21
  77.9 0.1 collective-permute-start.20
  78.0 0.5 collective-permute-done.14.refs_0_
  78.5 3.1 %collective-permute-start.15 = (bf16[128,1536]{1,0:T(8,128)(2,1)S(1)}, bf16[128,1536]{1,0:T(8,128)(2,1)S(1)}, u32[]{:S(2)}, u32[]{:S(2)}) collective-permute-start(bf16[128,1536]{1,0:T(8,128)(2,1)S(1)} %collective-permute-done.14.refs_0_), channel_id=1, source_target_pairs={{0,32},{16,240},{32,64},{48,16},{64,96},{80,48},{96,128},{112,80},... | collective-permute-start | bytes 1179656 | tf_op jit(solution)/shard_map/ppermute | solution.py:149
  81.6 1.1 collective-permute-done.6.refs_0_
  82.7 3.1 %collective-permute-start.7 = (bf16[128,1536]{1,0:T(8,128)(2,1)S(1)}, bf16[128,1536]{1,0:T(8,128)(2,1)S(1)}, u32[]{:S(2)}, u32[]{:S(2)}) collective-permute-start(bf16[128,1536]{1,0:T(8,128)(2,1)S(1)} %collective-permute-done.6.refs_0_), channel_id=1, source_target_pairs={{0,32},{16,240},{32,64},{48,16},{64,96},{80,48},{96,128},{112,80},... | collective-permute-start | bytes 1179656 | tf_op jit(solution)/shard_map/ppermute | solution.py:150
  85.8 0.5 collective-permute-start.18
  86.3 0.1 collective-permute-start.17
  86.4 0.5 collective-permute-done.15.refs_0_
  86.9 2.7 %collective-permute-start.16 = (bf16[128,1536]{1,0:T(8,128)(2,1)S(1)}, bf16[128,1536]{1,0:T(8,128)(2,1)S(1)}, u32[]{:S(2)}, u32[]{:S(2)}) collective-permute-start(bf16[128,1536]{1,0:T(8,128)(2,1)S(1)} %collective-permute-done.15.refs_0_), channel_id=1, source_target_pairs={{0,16},{16,0},{32,48},{48,32},{64,80},{80,64},{96,112},{112,96},{1... | collective-permute-start | bytes 1179656 | tf_op jit(solution)/shard_map/ppermute | solution.py:137
  89.6 1.5 %collective-permute-done.7.refs_0_ = bf16[128,1536]{1,0:T(8,128)(2,1)S(1)} collective-permute-done((bf16[128,1536]{1,0:T(8,128)(2,1)S(1)}, bf16[128,1536]{1,0:T(8,128)(2,1)S(1)}, u32[]{:S(2)}, u32[]{:S(2)}) %collective-permute-start.7) | collective-permute-done | bytes 393248 | tf_op jit(solution)/shard_map/ppermute | solution.py:150
  91.1 2.7 %collective-permute-start.8 = (bf16[128,1536]{1,0:T(8,128)(2,1)S(1)}, bf16[128,1536]{1,0:T(8,128)(2,1)S(1)}, u32[]{:S(2)}, u32[]{:S(2)}) collective-permute-start(bf16[128,1536]{1,0:T(8,128)(2,1)S(1)} %collective-permute-done.7.refs_0_), channel_id=1, source_target_pairs={{0,16},{16,0},{32,48},{48,32},{64,80},{80,64},{96,112},{112,96},{1... | collective-permute-start | bytes 1179656 | tf_op jit(solution)/shard_map/ppermute | solution.py:137
  93.8 0.6 add_bitcast_fusion
  94.4 0.9 place.16
  95.3 0.9 place.17
  96.3 0.9 place.18
  97.2 0.9 place.19
  98.2 1.0 place.20
  99.2 1.0 place.21
  100.1 1.0 place.22
  101.1 1.0 place.23
  102.0 1.0 place.24
  103.0 1.0 place.25
  104.0 1.0 place.26
  104.9 1.0 place.27
  105.9 1.0 place.28
  106.9 1.0 place.29
  107.8 1.0 place.30
  108.8 1.0 place.31
  (45 shorter events, 0.1 us)
Async XLA Ops:
  0.6 1.9 %copy-start.7 = (f32[64]{0:T(128)S(1)}, f32[64]{0:T(128)}, u32[]{:S(2)}) copy-start(f32[64]{0:T(128)} %param.14) | copy-start | bytes 772
  0.7 1.9 %copy-start.8 = (f32[64]{0:T(128)S(1)}, f32[64]{0:T(128)}, u32[]{:S(2)}) copy-start(f32[64]{0:T(128)} %param.15) | copy-start | bytes 772
  0.7 1.9 %copy-start.5 = (f32[256,256]{1,0:T(8,128)S(1)}, f32[256,256]{1,0:T(8,128)}, u32[]{:S(2)}) copy-start(f32[256,256]{1,0:T(8,128)} %param.10) | copy-start | bytes 786436
  0.7 1.9 %copy-start.6 = (f32[256,256]{1,0:T(8,128)S(1)}, f32[256,256]{1,0:T(8,128)}, u32[]{:S(2)}) copy-start(f32[256,256]{1,0:T(8,128)} %param.11) | copy-start | bytes 786436
  0.7 1.9 %copy-start.3 = (f32[256,256]{1,0:T(8,128)S(1)}, f32[256,256]{1,0:T(8,128)}, u32[]{:S(2)}) copy-start(f32[256,256]{1,0:T(8,128)} %param.12) | copy-start | bytes 786436
  0.7 1.9 %copy-start.4 = (f32[256,256]{1,0:T(8,128)S(1)}, f32[256,256]{1,0:T(8,128)}, u32[]{:S(2)}) copy-start(f32[256,256]{1,0:T(8,128)} %param.13) | copy-start | bytes 786436
  2.6 92.7 %copy-start = (f32[256,1024]{1,0:T(8,128)}, f32[256,1024]{1,0:T(8,128)S(1)}, u32[]{:S(2)}) copy-start(f32[256,1024]{1,0:T(8,128)S(1)} %get-tuple-element.119.query) | copy-start | bytes 3145732
  2.7 93.5 %copy-start.1 = (f32[256,256]{1,0:T(8,128)}, f32[256,256]{1,0:T(8,128)S(1)}, u32[]{:S(2)}) copy-start(f32[256,256]{1,0:T(8,128)S(1)} %get-tuple-element.123.value) | copy-start | bytes 786436
  2.8 93.5 %copy-start.2 = (f32[256,256]{1,0:T(8,128)}, f32[256,256]{1,0:T(8,128)S(1)}, u32[]{:S(2)}) copy-start(f32[256,256]{1,0:T(8,128)S(1)} %get-tuple-element.125.key) | copy-start | bytes 786436
  21.9 1.7 %collective-permute-start = (bf16[128,1536]{1,0:T(8,128)(2,1)S(1)}, bf16[128,1536]{1,0:T(8,128)(2,1)S(1)}, u32[]{:S(2)}, u32[]{:S(2)}) collective-permute-start(bf16[128,1536]{1,0:T(8,128)(2,1)S(1)} %get-tuple-element.64.refs_1_), channel_id=1, source_target_pairs={{0,16},{16,0},{32,48},{48,32},{64,80},{80,64},{96,112},{112,96},{1... | collective-permute-start | bytes 1179656 | tf_op jit(solution)/shard_map/ppermute | solution.py:137
  21.9 6.9 %collective-permute-start.9 = (bf16[128,1536]{1,0:T(8,128)(2,1)S(1)}, bf16[128,1536]{1,0:T(8,128)(2,1)S(1)}, u32[]{:S(2)}, u32[]{:S(2)}) collective-permute-start(bf16[128,1536]{1,0:T(8,128)(2,1)S(1)} %get-tuple-element.65.refs_0_), channel_id=1, source_target_pairs={{0,32},{16,240},{32,64},{48,16},{64,96},{80,48},{96,128},{112,80},... | collective-permute-start | bytes 1179656 | tf_op jit(solution)/shard_map/ppermute | solution.py:149
  23.6 9.4 %collective-permute-start.1 = (bf16[128,1536]{1,0:T(8,128)(2,1)S(1)}, bf16[128,1536]{1,0:T(8,128)(2,1)S(1)}, u32[]{:S(2)}, u32[]{:S(2)}) collective-permute-start(bf16[128,1536]{1,0:T(8,128)(2,1)S(1)} %collective-permute-done.refs_0_), channel_id=1, source_target_pairs={{0,32},{16,240},{32,64},{48,16},{64,96},{80,48},{96,128},{112,80},... | collective-permute-start | bytes 1179656 | tf_op jit(solution)/shard_map/ppermute | solution.py:150
  28.8 8.4 %collective-permute-start.10 = (bf16[128,1536]{1,0:T(8,128)(2,1)S(1)}, bf16[128,1536]{1,0:T(8,128)(2,1)S(1)}, u32[]{:S(2)}, u32[]{:S(2)}) collective-permute-start(bf16[128,1536]{1,0:T(8,128)(2,1)S(1)} %collective-permute-done.9.refs_0_), channel_id=1, source_target_pairs={{0,32},{16,240},{32,64},{48,16},{64,96},{80,48},{96,128},{112,80},... | collective-permute-start | bytes 1179656 | tf_op jit(solution)/shard_map/ppermute | solution.py:149
  33.0 8.4 %collective-permute-start.2 = (bf16[128,1536]{1,0:T(8,128)(2,1)S(1)}, bf16[128,1536]{1,0:T(8,128)(2,1)S(1)}, u32[]{:S(2)}, u32[]{:S(2)}) collective-permute-start(bf16[128,1536]{1,0:T(8,128)(2,1)S(1)} %collective-permute-done.1.refs_0_), channel_id=1, source_target_pairs={{0,32},{16,240},{32,64},{48,16},{64,96},{80,48},{96,128},{112,80},... | collective-permute-start | bytes 1179656 | tf_op jit(solution)/shard_map/ppermute | solution.py:150
  37.2 8.4 %collective-permute-start.11 = (bf16[128,1536]{1,0:T(8,128)(2,1)S(1)}, bf16[128,1536]{1,0:T(8,128)(2,1)S(1)}, u32[]{:S(2)}, u32[]{:S(2)}) collective-permute-start(bf16[128,1536]{1,0:T(8,128)(2,1)S(1)} %collective-permute-done.10.refs_0_), channel_id=1, source_target_pairs={{0,32},{16,240},{32,64},{48,16},{64,96},{80,48},{96,128},{112,80},... | collective-permute-start | bytes 1179656 | tf_op jit(solution)/shard_map/ppermute | solution.py:149
  41.4 8.4 %collective-permute-start.3 = (bf16[128,1536]{1,0:T(8,128)(2,1)S(1)}, bf16[128,1536]{1,0:T(8,128)(2,1)S(1)}, u32[]{:S(2)}, u32[]{:S(2)}) collective-permute-start(bf16[128,1536]{1,0:T(8,128)(2,1)S(1)} %collective-permute-done.2.refs_0_), channel_id=1, source_target_pairs={{0,32},{16,240},{32,64},{48,16},{64,96},{80,48},{96,128},{112,80},... | collective-permute-start | bytes 1179656 | tf_op jit(solution)/shard_map/ppermute | solution.py:150
  42.4 19.7 %collective-permute-start.29 = (bf16[128,1536]{1,0:T(8,128)(2,1)S(1)}, bf16[128,1536]{1,0:T(8,128)(2,1)S(1)}, u32[]{:S(2)}, u32[]{:S(2)}) collective-permute-start(bf16[128,1536]{1,0:T(8,128)(2,1)S(1)} %get-tuple-element.65.refs_0_), channel_id=1, source_target_pairs={{0,16},{16,0},{32,48},{48,32},{64,80},{80,64},{96,112},{112,96},{1... | collective-permute-start | bytes 1179656 | tf_op jit(solution)/shard_map/ppermute | solution.py:137
  45.7 16.4 %collective-permute-start.12 = (bf16[128,1536]{1,0:T(8,128)(2,1)S(1)}, bf16[128,1536]{1,0:T(8,128)(2,1)S(1)}, u32[]{:S(2)}, u32[]{:S(2)}) collective-permute-start(bf16[128,1536]{1,0:T(8,128)(2,1)S(1)} %collective-permute-done.11.refs_0_), channel_id=1, source_target_pairs={{0,32},{16,240},{32,64},{48,16},{64,96},{80,48},{96,128},{112,80},... | collective-permute-start | bytes 1179656 | tf_op jit(solution)/shard_map/ppermute | solution.py:149
  49.9 15.4 %collective-permute-start.4 = (bf16[128,1536]{1,0:T(8,128)(2,1)S(1)}, bf16[128,1536]{1,0:T(8,128)(2,1)S(1)}, u32[]{:S(2)}, u32[]{:S(2)}) collective-permute-start(bf16[128,1536]{1,0:T(8,128)(2,1)S(1)} %collective-permute-done.3.refs_0_), channel_id=1, source_target_pairs={{0,32},{16,240},{32,64},{48,16},{64,96},{80,48},{96,128},{112,80},... | collective-permute-start | bytes 1179656 | tf_op jit(solution)/shard_map/ppermute | solution.py:150
  50.8 4.0 %collective-permute-start.30 = (bf16[32,128]{1,0:T(8,128)(2,1)S(1)}, bf16[32,128]{1,0:T(8,128)(2,1)S(1)}, u32[]{:S(2)}, u32[]{:S(2)}) collective-permute-start(bf16[32,128]{1,0:T(8,128)(2,1)S(1)} %get-tuple-element.117), channel_id=1, source_target_pairs={{0,4},{4,8},{8,12},{12,0},{1,5},{5,9},{9,13},{13,1},{2,6},{6,10},{... | collective-permute-start | bytes 24584 | tf_op jit(solution)/shard_map/ppermute | solution.py:170
  52.0 4.0 %collective-permute-start.31 = (bf16[32,128]{1,0:T(8,128)(2,1)S(1)}, bf16[32,128]{1,0:T(8,128)(2,1)S(1)}, u32[]{:S(2)}, u32[]{:S(2)}) collective-permute-start(bf16[32,128]{1,0:T(8,128)(2,1)S(1)} %get-tuple-element.117), channel_id=1, source_target_pairs={{0,8},{4,12},{8,0},{12,4},{1,9},{5,13},{9,1},{13,5},{2,10},{6,14},... | collective-permute-start | bytes 24584 | tf_op jit(solution)/shard_map/ppermute | solution.py:170
  54.8 5.4 %collective-permute-start.32 = (bf16[32,128]{1,0:T(8,128)(2,1)S(1)}, bf16[32,128]{1,0:T(8,128)(2,1)S(1)}, u32[]{:S(2)}, u32[]{:S(2)}) collective-permute-start(bf16[32,128]{1,0:T(8,128)(2,1)S(1)} %get-tuple-element.117), channel_id=1, source_target_pairs={{0,12},{4,0},{8,4},{12,8},{1,13},{5,1},{9,5},{13,9},{2,14},{6,2},{... | collective-permute-start | bytes 24584 | tf_op jit(solution)/shard_map/ppermute | solution.py:170
  56.0 9.4 %collective-permute-start.28 = (bf16[128,1536]{1,0:T(8,128)(2,1)S(1)}, bf16[128,1536]{1,0:T(8,128)(2,1)S(1)}, u32[]{:S(2)}, u32[]{:S(2)}) collective-permute-start(bf16[128,1536]{1,0:T(8,128)(2,1)S(1)} %collective-permute-done.9.refs_0_), channel_id=1, source_target_pairs={{0,16},{16,0},{32,48},{48,32},{64,80},{80,64},{96,112},{112,96},{1... | collective-permute-start | bytes 1179656 | tf_op jit(solution)/shard_map/ppermute | solution.py:137
  60.2 5.2 %collective-permute-start.27 = (bf16[128,1536]{1,0:T(8,128)(2,1)S(1)}, bf16[128,1536]{1,0:T(8,128)(2,1)S(1)}, u32[]{:S(2)}, u32[]{:S(2)}) collective-permute-start(bf16[128,1536]{1,0:T(8,128)(2,1)S(1)} %collective-permute-done.1.refs_0_), channel_id=1, source_target_pairs={{0,16},{16,0},{32,48},{48,32},{64,80},{80,64},{96,112},{112,96},{1... | collective-permute-start | bytes 1179656 | tf_op jit(solution)/shard_map/ppermute | solution.py:137
  62.1 3.8 %collective-permute-start.26 = (bf16[128,1536]{1,0:T(8,128)(2,1)S(1)}, bf16[128,1536]{1,0:T(8,128)(2,1)S(1)}, u32[]{:S(2)}, u32[]{:S(2)}) collective-permute-start(bf16[128,1536]{1,0:T(8,128)(2,1)S(1)} %collective-permute-done.10.refs_0_), channel_id=1, source_target_pairs={{0,16},{16,0},{32,48},{48,32},{64,80},{80,64},{96,112},{112,96},{1... | collective-permute-start | bytes 1179656 | tf_op jit(solution)/shard_map/ppermute | solution.py:137
  62.1 7.9 %collective-permute-start.13 = (bf16[128,1536]{1,0:T(8,128)(2,1)S(1)}, bf16[128,1536]{1,0:T(8,128)(2,1)S(1)}, u32[]{:S(2)}, u32[]{:S(2)}) collective-permute-start(bf16[128,1536]{1,0:T(8,128)(2,1)S(1)} %collective-permute-done.12.refs_0_), channel_id=1, source_target_pairs={{0,32},{16,240},{32,64},{48,16},{64,96},{80,48},{96,128},{112,80},... | collective-permute-start | bytes 1179656 | tf_op jit(solution)/shard_map/ppermute | solution.py:149
  65.3 8.9 %collective-permute-start.5 = (bf16[128,1536]{1,0:T(8,128)(2,1)S(1)}, bf16[128,1536]{1,0:T(8,128)(2,1)S(1)}, u32[]{:S(2)}, u32[]{:S(2)}) collective-permute-start(bf16[128,1536]{1,0:T(8,128)(2,1)S(1)} %collective-permute-done.4.refs_0_), channel_id=1, source_target_pairs={{0,32},{16,240},{32,64},{48,16},{64,96},{80,48},{96,128},{112,80},... | collective-permute-start | bytes 1179656 | tf_op jit(solution)/shard_map/ppermute | solution.py:150
  65.4 12.0 %collective-permute-start.25 = (bf16[128,1536]{1,0:T(8,128)(2,1)S(1)}, bf16[128,1536]{1,0:T(8,128)(2,1)S(1)}, u32[]{:S(2)}, u32[]{:S(2)}) collective-permute-start(bf16[128,1536]{1,0:T(8,128)(2,1)S(1)} %collective-permute-done.2.refs_0_), channel_id=1, source_target_pairs={{0,16},{16,0},{32,48},{48,32},{64,80},{80,64},{96,112},{112,96},{1... | collective-permute-start | bytes 1179656 | tf_op jit(solution)/shard_map/ppermute | solution.py:137
  65.4 11.9 %collective-permute-start.24 = (bf16[128,1536]{1,0:T(8,128)(2,1)S(1)}, bf16[128,1536]{1,0:T(8,128)(2,1)S(1)}, u32[]{:S(2)}, u32[]{:S(2)}) collective-permute-start(bf16[128,1536]{1,0:T(8,128)(2,1)S(1)} %collective-permute-done.11.refs_0_), channel_id=1, source_target_pairs={{0,16},{16,0},{32,48},{48,32},{64,80},{80,64},{96,112},{112,96},{1... | collective-permute-start | bytes 1179656 | tf_op jit(solution)/shard_map/ppermute | solution.py:137
  65.9 12.0 %collective-permute-start.23 = (bf16[128,1536]{1,0:T(8,128)(2,1)S(1)}, bf16[128,1536]{1,0:T(8,128)(2,1)S(1)}, u32[]{:S(2)}, u32[]{:S(2)}) collective-permute-start(bf16[128,1536]{1,0:T(8,128)(2,1)S(1)} %collective-permute-done.3.refs_0_), channel_id=1, source_target_pairs={{0,16},{16,0},{32,48},{48,32},{64,80},{80,64},{96,112},{112,96},{1... | collective-permute-start | bytes 1179656 | tf_op jit(solution)/shard_map/ppermute | solution.py:137
  70.0 8.4 %collective-permute-start.14 = (bf16[128,1536]{1,0:T(8,128)(2,1)S(1)}, bf16[128,1536]{1,0:T(8,128)(2,1)S(1)}, u32[]{:S(2)}, u32[]{:S(2)}) collective-permute-start(bf16[128,1536]{1,0:T(8,128)(2,1)S(1)} %collective-permute-done.13.refs_0_), channel_id=1, source_target_pairs={{0,32},{16,240},{32,64},{48,16},{64,96},{80,48},{96,128},{112,80},... | collective-permute-start | bytes 1179656 | tf_op jit(solution)/shard_map/ppermute | solution.py:149
  74.2 8.4 %collective-permute-start.6 = (bf16[128,1536]{1,0:T(8,128)(2,1)S(1)}, bf16[128,1536]{1,0:T(8,128)(2,1)S(1)}, u32[]{:S(2)}, u32[]{:S(2)}) collective-permute-start(bf16[128,1536]{1,0:T(8,128)(2,1)S(1)} %collective-permute-done.5.refs_0_), channel_id=1, source_target_pairs={{0,32},{16,240},{32,64},{48,16},{64,96},{80,48},{96,128},{112,80},... | collective-permute-start | bytes 1179656 | tf_op jit(solution)/shard_map/ppermute | solution.py:150
  77.4 8.4 %collective-permute-start.22 = (bf16[128,1536]{1,0:T(8,128)(2,1)S(1)}, bf16[128,1536]{1,0:T(8,128)(2,1)S(1)}, u32[]{:S(2)}, u32[]{:S(2)}) collective-permute-start(bf16[128,1536]{1,0:T(8,128)(2,1)S(1)} %collective-permute-done.12.refs_0_), channel_id=1, source_target_pairs={{0,16},{16,0},{32,48},{48,32},{64,80},{80,64},{96,112},{112,96},{1... | collective-permute-start | bytes 1179656 | tf_op jit(solution)/shard_map/ppermute | solution.py:137
  77.4 8.4 %collective-permute-start.21 = (bf16[128,1536]{1,0:T(8,128)(2,1)S(1)}, bf16[128,1536]{1,0:T(8,128)(2,1)S(1)}, u32[]{:S(2)}, u32[]{:S(2)}) collective-permute-start(bf16[128,1536]{1,0:T(8,128)(2,1)S(1)} %collective-permute-done.4.refs_0_), channel_id=1, source_target_pairs={{0,16},{16,0},{32,48},{48,32},{64,80},{80,64},{96,112},{112,96},{1... | collective-permute-start | bytes 1179656 | tf_op jit(solution)/shard_map/ppermute | solution.py:137
  77.9 8.4 %collective-permute-start.20 = (bf16[128,1536]{1,0:T(8,128)(2,1)S(1)}, bf16[128,1536]{1,0:T(8,128)(2,1)S(1)}, u32[]{:S(2)}, u32[]{:S(2)}) collective-permute-start(bf16[128,1536]{1,0:T(8,128)(2,1)S(1)} %collective-permute-done.13.refs_0_), channel_id=1, source_target_pairs={{0,16},{16,0},{32,48},{48,32},{64,80},{80,64},{96,112},{112,96},{1... | collective-permute-start | bytes 1179656 | tf_op jit(solution)/shard_map/ppermute | solution.py:137
  78.5 8.4 %collective-permute-start.15 = (bf16[128,1536]{1,0:T(8,128)(2,1)S(1)}, bf16[128,1536]{1,0:T(8,128)(2,1)S(1)}, u32[]{:S(2)}, u32[]{:S(2)}) collective-permute-start(bf16[128,1536]{1,0:T(8,128)(2,1)S(1)} %collective-permute-done.14.refs_0_), channel_id=1, source_target_pairs={{0,32},{16,240},{32,64},{48,16},{64,96},{80,48},{96,128},{112,80},... | collective-permute-start | bytes 1179656 | tf_op jit(solution)/shard_map/ppermute | solution.py:149
  82.7 8.4 %collective-permute-start.7 = (bf16[128,1536]{1,0:T(8,128)(2,1)S(1)}, bf16[128,1536]{1,0:T(8,128)(2,1)S(1)}, u32[]{:S(2)}, u32[]{:S(2)}) collective-permute-start(bf16[128,1536]{1,0:T(8,128)(2,1)S(1)} %collective-permute-done.6.refs_0_), channel_id=1, source_target_pairs={{0,32},{16,240},{32,64},{48,16},{64,96},{80,48},{96,128},{112,80},... | collective-permute-start | bytes 1179656 | tf_op jit(solution)/shard_map/ppermute | solution.py:150
  85.8 19.1 %collective-permute-start.19 = (bf16[128,1536]{1,0:T(8,128)(2,1)S(1)}, bf16[128,1536]{1,0:T(8,128)(2,1)S(1)}, u32[]{:S(2)}, u32[]{:S(2)}) collective-permute-start(bf16[128,1536]{1,0:T(8,128)(2,1)S(1)} %collective-permute-done.5.refs_0_), channel_id=1, source_target_pairs={{0,16},{16,0},{32,48},{48,32},{64,80},{80,64},{96,112},{112,96},{1... | collective-permute-start | bytes 1179656 | tf_op jit(solution)/shard_map/ppermute | solution.py:137
  85.8 20.1 %collective-permute-start.18 = (bf16[128,1536]{1,0:T(8,128)(2,1)S(1)}, bf16[128,1536]{1,0:T(8,128)(2,1)S(1)}, u32[]{:S(2)}, u32[]{:S(2)}) collective-permute-start(bf16[128,1536]{1,0:T(8,128)(2,1)S(1)} %collective-permute-done.14.refs_0_), channel_id=1, source_target_pairs={{0,16},{16,0},{32,48},{48,32},{64,80},{80,64},{96,112},{112,96},{1... | collective-permute-start | bytes 1179656 | tf_op jit(solution)/shard_map/ppermute | solution.py:137
  86.3 20.6 %collective-permute-start.17 = (bf16[128,1536]{1,0:T(8,128)(2,1)S(1)}, bf16[128,1536]{1,0:T(8,128)(2,1)S(1)}, u32[]{:S(2)}, u32[]{:S(2)}) collective-permute-start(bf16[128,1536]{1,0:T(8,128)(2,1)S(1)} %collective-permute-done.6.refs_0_), channel_id=1, source_target_pairs={{0,16},{16,0},{32,48},{48,32},{64,80},{80,64},{96,112},{112,96},{1... | collective-permute-start | bytes 1179656 | tf_op jit(solution)/shard_map/ppermute | solution.py:137
  86.9 20.9 %collective-permute-start.16 = (bf16[128,1536]{1,0:T(8,128)(2,1)S(1)}, bf16[128,1536]{1,0:T(8,128)(2,1)S(1)}, u32[]{:S(2)}, u32[]{:S(2)}) collective-permute-start(bf16[128,1536]{1,0:T(8,128)(2,1)S(1)} %collective-permute-done.15.refs_0_), channel_id=1, source_target_pairs={{0,16},{16,0},{32,48},{48,32},{64,80},{80,64},{96,112},{112,96},{1... | collective-permute-start | bytes 1179656 | tf_op jit(solution)/shard_map/ppermute | solution.py:137
  91.1 17.7 %collective-permute-start.8 = (bf16[128,1536]{1,0:T(8,128)(2,1)S(1)}, bf16[128,1536]{1,0:T(8,128)(2,1)S(1)}, u32[]{:S(2)}, u32[]{:S(2)}) collective-permute-start(bf16[128,1536]{1,0:T(8,128)(2,1)S(1)} %collective-permute-done.7.refs_0_), channel_id=1, source_target_pairs={{0,16},{16,0},{32,48},{48,32},{64,80},{80,64},{96,112},{112,96},{1... | collective-permute-start | bytes 1179656 | tf_op jit(solution)/shard_map/ppermute | solution.py:137
where the time goes:
time: 110 us
  starting transfers between devices  42.3 us (38%)
  waiting for transfers between devices  29.5 us (27%)
  blocking collectives  18.4 us (17%)
  Pallas kernels  15.8 us (14%)
  other arithmetic  2.57 us (2%)
  between operations  1.19 us (1%)
    all_to_all x1, blocking collectives, body(): lax.all_to_all(copies, 'zero', split_axis=0, concat_axis=0, tiled=True)  18.4 us
    ppermute x16, starting transfers between devices, swap(): return lax.ppermute(piece, 'zero', other_core())  15.5 us
    pallas_call x16, Pallas kernels, placed(): pl.pallas_call(functools.partial(place, spots), out_shape=shapes, in_spec...  15.2 us
    ppermute x7, waiting for transfers between devices, body(): near = lax.ppermute(near, 'zero', both_ways())  14.5 us
    ppermute x7, starting transfers between devices, body(): near = lax.ppermute(near, 'zero', both_ways())  13.2 us
    ppermute x7, waiting for transfers between devices, body(): far = lax.ppermute(far, 'zero', both_ways())  12.6 us
    ppermute x7, starting transfers between devices, body(): far = lax.ppermute(far, 'zero', both_ways())  9.09 us
    ppermute x3, starting transfers between devices, body(): theirs = lax.ppermute(gains, 'tp', [(i, (i + k) % tp) for i in range(tp)])  4.63 us
  transfers between devices with their start and end apart: 33, of which 15 were waited for; matrix products, arithmetic and copies ran while one was open for 1% of the time, Pallas kernels for 13%

commit v1 on v0

--- a/solution.py
+++ b/solution.py
@@ -11,6 +11,7 @@
 keep_rate = 0.75
 CHIPS = 8
 CORES = 2
+LAST = CHIPS - 1
 
 
 def both_ways():
@@ -23,24 +24,84 @@
     return [(z * CORES + c, z * CORES + 1 - c) for z in range(CHIPS) for c in range(CORES)]
 
 
+def pack(query, key, value, out):
+    wide, narrow, half = query.shape[1], key.shape[1], query.shape[0] // CORES
+    at = pl.ds(pl.multiple_of(lax.axis_index("zero") % CORES * half, half), out.shape[0])
+    out[:, :wide] = query[at]
+    out[:, wide : wide + narrow] = key[at]
+    out[:, wide + narrow :] = value[at]
+
+
+def join(*refs):
+    *parts, line = refs
+    at = 0
+    for part in parts:
+        line[:, at : at + part.shape[1]] = part[...]
+        at += part.shape[1]
+
+
+def stack(first, second, out):
+    rows = first.shape[0]
+    out[:rows] = first[...]
+    out[rows:] = second[...]
+
+
+def stacked(first, second):
+    vm = pl.BlockSpec(memory_space=pltpu.VMEM)
+    return pl.pallas_call(
+        stack,
+        out_shape=pltpu.VMEM((2 * first.shape[0], first.shape[1]), first.dtype),
+        in_specs=[vm] * 2,
+        out_specs=vm,
+        compiler_params=pltpu.CompilerParams(vmem_limit_bytes=1 << 20),
+        name="stack",
+    )(*(pltpu.with_memory_space_constraint(a, pltpu.VMEM) for a in (first, second)))
+
+
+def tick(*refs):
+    del refs
+
+
+def ticked(outs):
+    where = [pl.BlockSpec(memory_space=pl.ANY)] * len(outs)
+    return pl.pallas_call(
+        tick,
+        out_shape=[jax.ShapeDtypeStruct(a.shape, a.dtype) for a in outs],
+        in_specs=where,
+        out_specs=where,
+        input_output_aliases={j: j for j in range(len(outs))},
+        compiler_params=pltpu.CompilerParams(vmem_limit_bytes=1 << 20),
+        name="tick",
+    )(*outs)
+
+
+def receive(early, column_query, column_key, column_value, out):
+    at = 0
+    for column in (column_query, column_key, column_value):
+        here = slice(at, at + column.shape[1])
+        out[:, here] = (early[:, here] / column[...]).astype(out.dtype)
+        at += column.shape[1]
+
+
 def normalise(everyone, query, key, value, *outs):
-    pieces, (column_query, column_key, column_value, gain) = outs[:2], outs[2:]
+    pieces, (late, *gives), columns, gain = outs[:2], outs[2:5], outs[5:11], outs[11]
     wide, narrow = query.shape[1], key.shape[1]
     total = jnp.sum(everyone[...], axis=0, keepdims=True)
     column = jnp.sqrt(total[:, : wide + 2 * narrow])
-    column_query[...] = column[:, :wide]
-    column_key[...] = column[:, wide : wide + narrow]
-    column_value[...] = column[:, wide + narrow :]
-    mine = lax.axis_index("tp")
+    for here in (columns[:3], columns[3:]):
+        here[0][...] = column[:, :wide]
+        here[1][...] = column[:, wide : wide + narrow]
+        here[2][...] = column[:, wide + narrow :]
+    tp = lax.axis_index("tp")
     own = everyone[:, wide + 2 * narrow :]
     size, each = own.shape
     twice = jnp.concatenate([own, own], axis=1).astype(jnp.bfloat16)
     tall = (2 * size, size)
     row, owner = (lax.broadcasted_iota(jnp.int32, tall, d) for d in (0, 1))
-    spread = (row == 2 * owner + mine // 2).astype(jnp.bfloat16)
+    spread = (row == 2 * owner + tp // 2).astype(jnp.bfloat16)
     moved = jnp.dot(spread, twice, preferred_element_type=jnp.float32)
     lane = lax.broadcasted_iota(jnp.int32, moved.shape, 1)
-    gain[...] = jnp.where(lane // each == mine % 2, moved, 0.0).astype(gain.dtype)
+    gain[...] = jnp.where(lane // each == tp % 2, moved, 0.0).astype(gain.dtype)
     rows = pieces[0].shape[0]
     core = lax.axis_index("zero") % CORES
     for piece, half in zip(pieces, (core, 1 - core)):
@@ -48,6 +109,10 @@
         piece[:, :wide] = (query[at] / column[:, :wide]).astype(piece.dtype)
         piece[:, wide : wide + narrow] = (key[at] / column[:, wide : wide + narrow]).astype(piece.dtype)
         piece[:, wide + narrow :] = (value[at] / column[:, wide + narrow :]).astype(piece.dtype)
+    half = late.shape[0]
+    late[...] = pieces[0][half:]
+    gives[0][...] = pieces[1][:half]
+    gives[1][...] = pieces[1][half:]
 
 
 def place(spots, *refs):
@@ -56,12 +121,13 @@
     me = lax.axis_index("zero")
     z, c = me // CORES, me % CORES
     copies = []
-    for k, (hops, theirs, other) in enumerate(spots):
+    for k, (hops, theirs, other, part) in enumerate(spots):
         rows = pieces[k].shape[0]
         half = 1 - c if theirs else c
         shard = 1 - c if other else c
         chip = (z - hops * (1 - 2 * half) + CHIPS) % CHIPS
-        row = pl.multiple_of(((chip * CORES + shard) * 2 + half) * rows, rows)
+        unit = outs[0].shape[0] // (CHIPS * CORES * 2)
+        row = pl.multiple_of(((chip * CORES + shard) * 2 + half) * unit + part * rows, rows)
         column = 0
         for j, out in enumerate(outs):
             wide = out.shape[1]
@@ -105,78 +171,123 @@
     depth, wide = fresh_query.shape
     narrow = fresh_key.shape[1]
     gain = (norm_train + norm_step).astype(jnp.bfloat16)
-    line = jnp.concatenate(
-        [
-            jnp.sum(fresh_query * fresh_query, axis=0),
-            jnp.sum(fresh_key * fresh_key, axis=0),
-            jnp.sum(fresh_value * fresh_value, axis=0),
-            gain.astype(jnp.float32),
-        ]
-    )
+    rows, full = depth // 2, wide + 2 * narrow
+    vm = pl.BlockSpec(memory_space=pltpu.VMEM)
+    fresh = [pltpu.with_memory_space_constraint(a, pltpu.VMEM) for a in (fresh_query, fresh_key, fresh_value)]
+    early = pl.pallas_call(
+        pack,
+        out_shape=pltpu.VMEM((rows // 2, full), jnp.float32),
+        in_specs=[vm] * 3,
+        out_specs=vm,
+        compiler_params=pltpu.CompilerParams(vmem_limit_bytes=8 << 20),
+        name="pack",
+    )(*fresh)
+    early = lax.ppermute(early, "zero", both_ways())
+    parts = [
+        *(jnp.sum(a * a, axis=0, keepdims=True) for a in (fresh_query, fresh_key, fresh_value)),
+        gain.astype(jnp.float32).reshape(1, -1),
+    ]
+    line = pl.pallas_call(
+        join,
+        out_shape=pltpu.VMEM((1, full + gain.size), jnp.float32),
+        in_specs=[vm] * 4,
+        out_specs=vm,
+        compiler_params=pltpu.CompilerParams(vmem_limit_bytes=1 << 20),
+        name="join",
+    )(*(pltpu.with_memory_space_constraint(a, pltpu.VMEM) for a in parts))
     copies = jnp.broadcast_to(line, (CHIPS * CORES, line.size))
     everyone = lax.all_to_all(copies, "zero", split_axis=0, concat_axis=0, tiled=True)
-
-    rows, full = depth // 2, wide + 2 * narrow
-    vm = pl.BlockSpec(memory_space=pltpu.VMEM)
-    keep, give, column_query, column_key, column_value, gains = pl.pallas_call(
+    keep, give, late, *gives, q, k, v, q_out, k_out, v_out, gains = pl.pallas_call(
         normalise,
         out_shape=[pltpu.VMEM((rows, full), jnp.bfloat16)] * 2
+        + [pltpu.VMEM((rows // 2, full), jnp.bfloat16)] * 3
+        + [pltpu.VMEM((1, n), jnp.float32) for n in (wide, narrow, narrow)]
         + [jax.ShapeDtypeStruct((1, n), jnp.float32) for n in (wide, narrow, narrow)]
         + [pltpu.VMEM((2 * CHIPS * CORES, 2 * gain.size), jnp.bfloat16)],
         in_specs=[vm] * 4,
-        out_specs=[vm] * 6,
+        out_specs=[vm] * 12,
         compiler_params=pltpu.CompilerParams(vmem_limit_bytes=8 << 20),
         name="normalise",
-    )(
-        everyone,
-        *(pltpu.with_memory_space_constraint(a, pltpu.VMEM) for a in (fresh_query, fresh_key, fresh_value)),
-    )
+    )(everyone, *fresh)
+    near = pl.pallas_call(
+        receive,
+        out_shape=pltpu.VMEM((rows // 2, full), jnp.bfloat16),
+        in_specs=[vm] * 4,
+        out_specs=vm,
+        compiler_params=pltpu.CompilerParams(vmem_limit_bytes=8 << 20),
+        name="receive",
+    )(*(pltpu.with_memory_space_constraint(a, pltpu.VMEM) for a in (early, q, k, v)))
 
     size = CHIPS * CORES
+
     def swap(piece):
         return lax.ppermute(piece, "zero", other_core())
 
-    near, far = keep, swap(give)
-    held = [
+    have = {("a", 1): near, ("b", 0): late}
+    have["c", 0], have["d", 0] = (swap(g) for g in gives)
+    for kind in "abcd":
+        for hop in range(1 + (kind == "a"), CHIPS):
+            have[kind, hop] = lax.ppermute(have[kind, hop - 1], "zero", both_ways())
+    hands = {"hand0": swap(keep)}
+    for hop in range(1, CHIPS):
+        for kind, pair in (("near", "ab"), ("far", "cd")):
+            if hop == LAST and kind == "far":
+                continue
+            both = stacked(*(have[p, hop] for p in pair))
+            hands[f"{kind}{hop}"] = swap(both)
+    for kind in "cd":
+        hands[f"{kind}{LAST}"] = swap(have[kind, LAST])
+
+    def mine(kind, hop):
+        return have[kind, hop], (hop, False, kind in "cd", "abcd".index(kind) % 2)
+
+    def theirs(kind, hop):
+        return hands[f"{kind}{hop}"], (hop, True, kind == "near", 0)
+
+    puts = [
         [
-            (keep, (0, False, False)),
-            (far, (0, False, True)),
-            (swap(keep), (0, True, True)),
-            (give, (0, True, False)),
+            (keep, (0, False, False, 0)),
+            (give, (0, True, False, 0)),
+            (have["c", 0], (0, False, True, 0)),
+            (have["d", 0], (0, False, True, 1)),
+        ],
+        [],
+        [mine("a", 1), mine("a", 2), mine("b", 1), (hands["hand0"], (0, True, True, 0))],
+        [],
+        [mine("c", 1), mine("d", 1)],
+    ]
+    for hop in range(2, LAST):
+        puts += [
+            [],
+            [mine("a", hop + 1), mine("b", hop), theirs("near", hop - 1), theirs("far", hop - 1)],
+            [],
+            [mine("c", hop), mine("d", hop)],
         ]
+    puts += [
+        [theirs("near", LAST - 1), theirs("far", LAST - 1)],
+        [mine("b", LAST)],
+        [theirs("near", LAST), mine("c", LAST)],
+        [(hands[f"c{LAST}"], (LAST, True, False, 0)), mine("d", LAST)],
+        [(hands[f"d{LAST}"], (LAST, True, False, 1))],
     ]
-    for hop in range(1, CHIPS):
-        near = lax.ppermute(near, "zero", both_ways())
-        far = lax.ppermute(far, "zero", both_ways())
-        held.append(
-            [
-                (near, (hop, False, False)),
-                (far, (hop, False, True)),
-                (swap(near), (hop, True, True)),
-                (swap(far), (hop, True, False)),
-            ]
-        )
 
     shapes = [jax.ShapeDtypeStruct((depth * size, n), jnp.bfloat16) for n in (wide, narrow, narrow)]
     outs = None
-    for some in held:
-        for two in (some[::2], some[1::2]):
-            outs = placed([p for p, _ in two], [s for _, s in two], outs, shapes)
+    for some in puts:
+        outs = placed([p for p, _ in some], [s for _, s in some], outs, shapes) if some else ticked(outs)
     serve_query, serve_key, serve_value = outs
 
     tp = lax.axis_size("tp")
     serve_norm = gains
-    for k in range(1, tp):
-        theirs = lax.ppermute(gains, "tp", [(i, (i + k) % tp) for i in range(tp)])
+    for k in (1, 2):
+        theirs = lax.ppermute(serve_norm, "tp", [(i, i ^ k) for i in range(tp)])
         serve_norm += theirs
     serve_norm = serve_norm.reshape(-1)
     return (
         serve_query,
         serve_key,
         serve_value,
-        column_query.reshape(-1),
-        column_key.reshape(-1),
-        column_value.reshape(-1),
+        *(column.reshape(-1) for column in (q_out, k_out, v_out)),
         serve_norm,
         fresh_query,
         fresh_key,

time: 110 us -> 121 us (1.10)
  starting transfers between devices: 42.3 us -> 86.8 us
  blocking collectives: 18.4 us -> 0 us
  waiting for transfers between devices: 29.5 us -> 11.6 us
  Pallas kernels: 15.8 us -> 17.9 us
    ppermute x17 -> x30, starting transfers between devices: 26.9 us -> 49.6 us  [the longest x27 43.3 us: body(): have[kind, hop] = lax.ppermute(have[kind, hop - 1], 'zero', both_ways())]
    ppermute x17 -> x30, waiting for transfers between devices: 27.8 us -> 5.55 us  [the longest x27 3.66 us: body(): have[kind, hop] = lax.ppermute(have[kind, hop - 1], 'zero', both_ways())]
    all_to_all x1 -> x0, blocking collectives: 18.4 us -> none  [body(): lax.all_to_all(copies, 'zero', split_axis=0, concat_axis=0, tiled=True)]
    ppermute x16 -> x18, starting transfers between devices: 15.5 us -> 27.2 us  [swap(): return lax.ppermute(piece, 'zero', other_core())]
    all_to_all x0 -> x1, starting transfers between devices: none -> 9.97 us  [body(): lax.all_to_all(copies, 'zero', split_axis=0, concat_axis=0, tiled=True)]
    all_to_all x0 -> x1, waiting for transfers between devices: none -> 5.96 us  [body(): lax.all_to_all(copies, 'zero', split_axis=0, concat_axis=0, tiled=True)]
    ppermute x16 -> x18, waiting for transfers between devices: 1.76 us -> 0.05 us  [swap(): return lax.ppermute(piece, 'zero', other_core())]
    pallas_call x16 -> x18, Pallas kernels: 15.2 us -> 16.8 us  [placed(): pl.pallas_call(functools.partial(place, spots), out_shape=shapes, in_spec...]
  transfers between devices with their start and end apart: 33 -> 49, of which waited for: 15 -> 9; matrix products, arithmetic and copies ran while one was open for 1% -> 1% of each run, Pallas kernels for 13% -> 14%
where the time goes in v1:
time: 121 us
  starting transfers between devices  86.8 us (72%)
  Pallas kernels  17.9 us (15%)
  waiting for transfers between devices  11.6 us (10%)
  other arithmetic  2.58 us (2%)
  between operations  1.45 us (1%)
    ppermute x27, starting transfers between devices, body(): have[kind, hop] = lax.ppermute(have[kind, hop - 1], 'zero', both_ways())  43.3 us
    ppermute x18, starting transfers between devices, swap(): return lax.ppermute(piece, 'zero', other_core())  27.2 us
    pallas_call x18, Pallas kernels, placed(): pl.pallas_call(functools.partial(place, spots), out_shape=shapes, in_spec...  16.8 us
    all_to_all x1, starting transfers between devices, body(): lax.all_to_all(copies, 'zero', split_axis=0, concat_axis=0, tiled=True)  9.97 us
    all_to_all x1, waiting for transfers between devices, body(): lax.all_to_all(copies, 'zero', split_axis=0, concat_axis=0, tiled=True)  5.96 us
    ppermute x27, waiting for transfers between devices, body(): have[kind, hop] = lax.ppermute(have[kind, hop - 1], 'zero', both_ways())  3.66 us
    ppermute x2, starting transfers between devices, body(): theirs = lax.ppermute(serve_norm, 'tp', [(i, i ^ k) for i in range(tp)])  3.66 us
    ppermute x1, starting transfers between devices, body(): early = lax.ppermute(early, 'zero', both_ways())  2.65 us
  transfers between devices with their start and end apart: 49, of which 9 were waited for; matrix products, arithmetic and copies ran while one was open for 1% of the time, Pallas kernels for 14%

profile of v1, /device:TPU:1, one launch (start us, length us, event | category | flops | bytes accessed | tf_op | source)
XLA Modules:
  0.0 121.3 jit_solution(12634385166571586121)
XLA Ops:
  0.7 1.8 %multiply_reduce_fusion = (f32[1024]{0:T(1024)S(1)}, f32[256,1024]{1,0:T(8,128)S(1)}) fusion(f32[256,1024]{1,0:T(8,128)} %param.8, f32[256,1024]{1,0:T(8,128)} %param.9), kind=kLoop, calls=%fused_computation | loop fusion | flops 1309696 | bytes 3149824 | tf_op jit(solution)/shard_map/reduce_sum | solution.py:187
  2.8 0.9 broadcast_in_dim.17
  3.7 10.0 %all-to-all-start = ((f32[16,1,1600]{2,1,0:T(1,128)}), f32[16,1,1600]{2,1,0:T(1,128)S(1)}, u32[]{:S(2)}, u32[]{:S(2)}) async-start(f32[16,1,1600]{2,1,0:T(1,128)} %broadcast_in_dim.17), calls=%async_computation | async-start | bytes 212992 | tf_op jit(solution)/shard_map/all_to_all | solution.py:199
  13.7 2.6 %collective-permute-start.18 = (f32[64,1536]{1,0:T(8,128)S(1)}, f32[64,1536]{1,0:T(8,128)S(1)}, u32[]{:S(2)}, u32[]{:S(2)}) collective-permute-start(f32[64,1536]{1,0:T(8,128)S(1)} %pack.1), channel_id=1, source_target_pairs={{0,32},{16,240},{32,64},{48,16},{64,96},{80,48},{96,128},{112,80},... | collective-permute-start | bytes 1179656 | tf_op jit(solution)/shard_map/ppermute | solution.py:185
  16.4 6.0 %all-to-all-done = f32[16,1,1600]{2,1,0:T(1,128)S(1)} async-done(((f32[16,1,1600]{2,1,0:T(1,128)}), f32[16,1,1600]{2,1,0:T(1,128)S(1)}, u32[]{:S(2)}, u32[]{:S(2)}) %all-to-all-start) | async-done | bytes 102432 | tf_op jit(solution)/shard_map/all_to_all | solution.py:199
  22.3 0.6 normalise.1
  23.6 1.2 collective-permute-start.46
  24.8 1.3 %collective-permute-done.46 = bf16[32,128]{1,0:T(8,128)(2,1)S(1)} collective-permute-done((bf16[32,128]{1,0:T(8,128)(2,1)S(1)}, bf16[32,128]{1,0:T(8,128)(2,1)S(1)}, u32[]{:S(2)}, u32[]{:S(2)}) %collective-permute-start.46) | collective-permute-done | bytes 8224 | tf_op jit(solution)/shard_map/ppermute | solution.py:283
  26.1 1.2 %collective-permute-start.45 = (bf16[128,1536]{1,0:T(8,128)(2,1)S(1)}, bf16[128,1536]{1,0:T(8,128)(2,1)S(1)}, u32[]{:S(2)}, u32[]{:S(2)}) collective-permute-start(bf16[128,1536]{1,0:T(8,128)(2,1)S(1)} %get-tuple-element.118.refs_0_), channel_id=1, source_target_pairs={{0,16},{16,0},{32,48},{48,32},{64,80},{80,64},{96,112},{112,96},{1... | collective-permute-start | bytes 1179656 | tf_op jit(solution)/shard_map/ppermute | solution.py:224
  27.4 0.8 collective-permute-start.1
  28.2 1.4 %collective-permute-done.25.second.refs_2_ = bf16[64,1536]{1,0:T(8,128)(2,1)S(1)} collective-permute-done((bf16[64,1536]{1,0:T(8,128)(2,1)S(1)}, bf16[64,1536]{1,0:T(8,128)(2,1)S(1)}, u32[]{:S(2)}, u32[]{:S(2)}) %collective-permute-start.25) | collective-permute-done | bytes 196640 | tf_op jit(solution)/shard_map/ppermute | solution.py:230
  29.6 2.5 %collective-permute-start.47 = (bf16[32,128]{1,0:T(8,128)(2,1)S(1)}, bf16[32,128]{1,0:T(8,128)(2,1)S(1)}, u32[]{:S(2)}, u32[]{:S(2)}) collective-permute-start(bf16[32,128]{1,0:T(8,128)(2,1)S(1)} %add.22), channel_id=1, source_target_pairs={{0,8},{4,12},{8,0},{12,4},{1,9},{5,13},{9,1},{13,5},{2,10},{6,14},... | collective-permute-start | bytes 24584 | tf_op jit(solution)/shard_map/ppermute | solution.py:283
  32.1 0.9 collective-permute-start.26
  33.6 0.9 collective-permute-start.19
  34.6 2.8 %collective-permute-start.43 = (bf16[128,1536]{1,0:T(8,128)(2,1)S(1)}, bf16[128,1536]{1,0:T(8,128)(2,1)S(1)}, u32[]{:S(2)}, u32[]{:S(2)}) collective-permute-start(bf16[128,1536]{1,0:T(8,128)(2,1)S(1)} %stack.24), channel_id=1, source_target_pairs={{0,16},{16,0},{32,48},{48,32},{64,80},{80,64},{96,112},{112,96},{1... | collective-permute-start | bytes 1179656 | tf_op jit(solution)/shard_map/ppermute | solution.py:224
  37.4 3.0 %collective-permute-start.11 = (bf16[64,1536]{1,0:T(8,128)(2,1)S(1)}, bf16[64,1536]{1,0:T(8,128)(2,1)S(1)}, u32[]{:S(2)}, u32[]{:S(2)}) collective-permute-start(bf16[64,1536]{1,0:T(8,128)(2,1)S(1)} %collective-permute-done.10.first.refs_0_), channel_id=1, source_target_pairs={{0,32},{16,240},{32,64},{48,16},{64,96},{80,48},{96,128},{112,80},... | collective-permute-start | bytes 589832 | tf_op jit(solution)/shard_map/ppermute | solution.py:230
  40.6 1.7 %collective-permute-start.27 = (bf16[64,1536]{1,0:T(8,128)(2,1)S(1)}, bf16[64,1536]{1,0:T(8,128)(2,1)S(1)}, u32[]{:S(2)}, u32[]{:S(2)}) collective-permute-start(bf16[64,1536]{1,0:T(8,128)(2,1)S(1)} %collective-permute-done.26.second.refs_1_), channel_id=1, source_target_pairs={{0,32},{16,240},{32,64},{48,16},{64,96},{80,48},{96,128},{112,80},... | collective-permute-start | bytes 589832 | tf_op jit(solution)/shard_map/ppermute | solution.py:230
  42.3 0.6 collective-permute-done.11.first.refs_0_
  42.9 3.1 %collective-permute-start.20 = (bf16[64,1536]{1,0:T(8,128)(2,1)S(1)}, bf16[64,1536]{1,0:T(8,128)(2,1)S(1)}, u32[]{:S(2)}, u32[]{:S(2)}) collective-permute-start(bf16[64,1536]{1,0:T(8,128)(2,1)S(1)} %collective-permute-done.19.first.refs_1_), channel_id=1, source_target_pairs={{0,32},{16,240},{32,64},{48,16},{64,96},{80,48},{96,128},{112,80},... | collective-permute-start | bytes 589832 | tf_op jit(solution)/shard_map/ppermute | solution.py:230
  46.1 2.5 %collective-permute-start.41 = (bf16[128,1536]{1,0:T(8,128)(2,1)S(1)}, bf16[128,1536]{1,0:T(8,128)(2,1)S(1)}, u32[]{:S(2)}, u32[]{:S(2)}) collective-permute-start(bf16[128,1536]{1,0:T(8,128)(2,1)S(1)} %stack.22), channel_id=1, source_target_pairs={{0,16},{16,0},{32,48},{48,32},{64,80},{80,64},{96,112},{112,96},{1... | collective-permute-start | bytes 1179656 | tf_op jit(solution)/shard_map/ppermute | solution.py:224
  48.6 1.7 %collective-permute-start.12 = (bf16[64,1536]{1,0:T(8,128)(2,1)S(1)}, bf16[64,1536]{1,0:T(8,128)(2,1)S(1)}, u32[]{:S(2)}, u32[]{:S(2)}) collective-permute-start(bf16[64,1536]{1,0:T(8,128)(2,1)S(1)} %collective-permute-done.11.first.refs_0_), channel_id=1, source_target_pairs={{0,32},{16,240},{32,64},{48,16},{64,96},{80,48},{96,128},{112,80},... | collective-permute-start | bytes 589832 | tf_op jit(solution)/shard_map/ppermute | solution.py:230
  50.3 0.8 collective-permute-start.42
  51.1 3.0 %collective-permute-start.3 = (bf16[64,1536]{1,0:T(8,128)(2,1)S(1)}, bf16[64,1536]{1,0:T(8,128)(2,1)S(1)}, u32[]{:S(2)}, u32[]{:S(2)}) collective-permute-start(bf16[64,1536]{1,0:T(8,128)(2,1)S(1)} %collective-permute-done.2.second.refs_1_), channel_id=1, source_target_pairs={{0,32},{16,240},{32,64},{48,16},{64,96},{80,48},{96,128},{112,80},... | collective-permute-start | bytes 589832 | tf_op jit(solution)/shard_map/ppermute | solution.py:230
  54.2 1.8 %collective-permute-start.21 = (bf16[64,1536]{1,0:T(8,128)(2,1)S(1)}, bf16[64,1536]{1,0:T(8,128)(2,1)S(1)}, u32[]{:S(2)}, u32[]{:S(2)}) collective-permute-start(bf16[64,1536]{1,0:T(8,128)(2,1)S(1)} %collective-permute-done.20.first.refs_0_), channel_id=1, source_target_pairs={{0,32},{16,240},{32,64},{48,16},{64,96},{80,48},{96,128},{112,80},... | collective-permute-start | bytes 589832 | tf_op jit(solution)/shard_map/ppermute | solution.py:230
  56.0 0.7 collective-permute-done.3.second.refs_1_
  56.7 3.3 %collective-permute-start.39 = (bf16[128,1536]{1,0:T(8,128)(2,1)S(1)}, bf16[128,1536]{1,0:T(8,128)(2,1)S(1)}, u32[]{:S(2)}, u32[]{:S(2)}) collective-permute-start(bf16[128,1536]{1,0:T(8,128)(2,1)S(1)} %stack.20), channel_id=1, source_target_pairs={{0,16},{16,0},{32,48},{48,32},{64,80},{80,64},{96,112},{112,96},{1... | collective-permute-start | bytes 1179656 | tf_op jit(solution)/shard_map/ppermute | solution.py:224
  60.0 1.9 %collective-permute-start.13 = (bf16[64,1536]{1,0:T(8,128)(2,1)S(1)}, bf16[64,1536]{1,0:T(8,128)(2,1)S(1)}, u32[]{:S(2)}, u32[]{:S(2)}) collective-permute-start(bf16[64,1536]{1,0:T(8,128)(2,1)S(1)} %collective-permute-done.12.first.refs_0_), channel_id=1, source_target_pairs={{0,32},{16,240},{32,64},{48,16},{64,96},{80,48},{96,128},{112,80},... | collective-permute-start | bytes 589832 | tf_op jit(solution)/shard_map/ppermute | solution.py:230
  62.2 3.0 %collective-permute-start.4 = (bf16[64,1536]{1,0:T(8,128)(2,1)S(1)}, bf16[64,1536]{1,0:T(8,128)(2,1)S(1)}, u32[]{:S(2)}, u32[]{:S(2)}) collective-permute-start(bf16[64,1536]{1,0:T(8,128)(2,1)S(1)} %collective-permute-done.3.second.refs_1_), channel_id=1, source_target_pairs={{0,32},{16,240},{32,64},{48,16},{64,96},{80,48},{96,128},{112,80},... | collective-permute-start | bytes 589832 | tf_op jit(solution)/shard_map/ppermute | solution.py:230
  65.3 2.4 %collective-permute-start.22 = (bf16[64,1536]{1,0:T(8,128)(2,1)S(1)}, bf16[64,1536]{1,0:T(8,128)(2,1)S(1)}, u32[]{:S(2)}, u32[]{:S(2)}) collective-permute-start(bf16[64,1536]{1,0:T(8,128)(2,1)S(1)} %collective-permute-done.21.first.refs_0_), channel_id=1, source_target_pairs={{0,32},{16,240},{32,64},{48,16},{64,96},{80,48},{96,128},{112,80},... | collective-permute-start | bytes 589832 | tf_op jit(solution)/shard_map/ppermute | solution.py:230
  67.8 3.8 %collective-permute-start.37 = (bf16[128,1536]{1,0:T(8,128)(2,1)S(1)}, bf16[128,1536]{1,0:T(8,128)(2,1)S(1)}, u32[]{:S(2)}, u32[]{:S(2)}) collective-permute-start(bf16[128,1536]{1,0:T(8,128)(2,1)S(1)} %stack.18), channel_id=1, source_target_pairs={{0,16},{16,0},{32,48},{48,32},{64,80},{80,64},{96,112},{112,96},{1... | collective-permute-start | bytes 1179656 | tf_op jit(solution)/shard_map/ppermute | solution.py:224
  71.6 1.4 %collective-permute-start.14 = (bf16[64,1536]{1,0:T(8,128)(2,1)S(1)}, bf16[64,1536]{1,0:T(8,128)(2,1)S(1)}, u32[]{:S(2)}, u32[]{:S(2)}) collective-permute-start(bf16[64,1536]{1,0:T(8,128)(2,1)S(1)} %collective-permute-done.13.first.refs_0_), channel_id=1, source_target_pairs={{0,32},{16,240},{32,64},{48,16},{64,96},{80,48},{96,128},{112,80},... | collective-permute-start | bytes 589832 | tf_op jit(solution)/shard_map/ppermute | solution.py:230
  73.0 0.8 collective-permute-start.38
  73.9 3.0 %collective-permute-start.5 = (bf16[64,1536]{1,0:T(8,128)(2,1)S(1)}, bf16[64,1536]{1,0:T(8,128)(2,1)S(1)}, u32[]{:S(2)}, u32[]{:S(2)}) collective-permute-start(bf16[64,1536]{1,0:T(8,128)(2,1)S(1)} %collective-permute-done.4.second.refs_1_), channel_id=1, source_target_pairs={{0,32},{16,240},{32,64},{48,16},{64,96},{80,48},{96,128},{112,80},... | collective-permute-start | bytes 589832 | tf_op jit(solution)/shard_map/ppermute | solution.py:230
  76.9 1.8 %collective-permute-start.23 = (bf16[64,1536]{1,0:T(8,128)(2,1)S(1)}, bf16[64,1536]{1,0:T(8,128)(2,1)S(1)}, u32[]{:S(2)}, u32[]{:S(2)}) collective-permute-start(bf16[64,1536]{1,0:T(8,128)(2,1)S(1)} %collective-permute-done.22.first.refs_0_), channel_id=1, source_target_pairs={{0,32},{16,240},{32,64},{48,16},{64,96},{80,48},{96,128},{112,80},... | collective-permute-start | bytes 589832 | tf_op jit(solution)/shard_map/ppermute | solution.py:230
  78.8 0.7 collective-permute-done.5.second.refs_1_
  79.4 3.3 %collective-permute-start.35 = (bf16[128,1536]{1,0:T(8,128)(2,1)S(1)}, bf16[128,1536]{1,0:T(8,128)(2,1)S(1)}, u32[]{:S(2)}, u32[]{:S(2)}) collective-permute-start(bf16[128,1536]{1,0:T(8,128)(2,1)S(1)} %stack.16), channel_id=1, source_target_pairs={{0,16},{16,0},{32,48},{48,32},{64,80},{80,64},{96,112},{112,96},{1... | collective-permute-start | bytes 1179656 | tf_op jit(solution)/shard_map/ppermute | solution.py:224
  82.7 1.9 %collective-permute-start.15 = (bf16[64,1536]{1,0:T(8,128)(2,1)S(1)}, bf16[64,1536]{1,0:T(8,128)(2,1)S(1)}, u32[]{:S(2)}, u32[]{:S(2)}) collective-permute-start(bf16[64,1536]{1,0:T(8,128)(2,1)S(1)} %collective-permute-done.14.first.refs_0_), channel_id=1, source_target_pairs={{0,32},{16,240},{32,64},{48,16},{64,96},{80,48},{96,128},{112,80},... | collective-permute-start | bytes 589832 | tf_op jit(solution)/shard_map/ppermute | solution.py:230
  85.0 3.0 %collective-permute-start.6 = (bf16[64,1536]{1,0:T(8,128)(2,1)S(1)}, bf16[64,1536]{1,0:T(8,128)(2,1)S(1)}, u32[]{:S(2)}, u32[]{:S(2)}) collective-permute-start(bf16[64,1536]{1,0:T(8,128)(2,1)S(1)} %collective-permute-done.5.second.refs_1_), channel_id=1, source_target_pairs={{0,32},{16,240},{32,64},{48,16},{64,96},{80,48},{96,128},{112,80},... | collective-permute-start | bytes 589832 | tf_op jit(solution)/shard_map/ppermute | solution.py:230
  88.0 2.4 %collective-permute-start.24 = (bf16[64,1536]{1,0:T(8,128)(2,1)S(1)}, bf16[64,1536]{1,0:T(8,128)(2,1)S(1)}, u32[]{:S(2)}, u32[]{:S(2)}) collective-permute-start(bf16[64,1536]{1,0:T(8,128)(2,1)S(1)} %collective-permute-done.23.first.refs_0_), channel_id=1, source_target_pairs={{0,32},{16,240},{32,64},{48,16},{64,96},{80,48},{96,128},{112,80},... | collective-permute-start | bytes 589832 | tf_op jit(solution)/shard_map/ppermute | solution.py:230
  90.5 3.1 %collective-permute-start.16 = (bf16[64,1536]{1,0:T(8,128)(2,1)S(1)}, bf16[64,1536]{1,0:T(8,128)(2,1)S(1)}, u32[]{:S(2)}, u32[]{:S(2)}) collective-permute-start(bf16[64,1536]{1,0:T(8,128)(2,1)S(1)} %collective-permute-done.15.first.refs_0_), channel_id=1, source_target_pairs={{0,32},{16,240},{32,64},{48,16},{64,96},{80,48},{96,128},{112,80},... | collective-permute-start | bytes 589832 | tf_op jit(solution)/shard_map/ppermute | solution.py:230
  93.7 2.1 %collective-permute-start.7 = (bf16[64,1536]{1,0:T(8,128)(2,1)S(1)}, bf16[64,1536]{1,0:T(8,128)(2,1)S(1)}, u32[]{:S(2)}, u32[]{:S(2)}) collective-permute-start(bf16[64,1536]{1,0:T(8,128)(2,1)S(1)} %collective-permute-done.6.second.refs_1_), channel_id=1, source_target_pairs={{0,32},{16,240},{32,64},{48,16},{64,96},{80,48},{96,128},{112,80},... | collective-permute-start | bytes 589832 | tf_op jit(solution)/shard_map/ppermute | solution.py:230
  95.8 0.8 collective-permute-start.33
  96.7 1.9 %collective-permute-start.34 = (bf16[128,1536]{1,0:T(8,128)(2,1)S(1)}, bf16[128,1536]{1,0:T(8,128)(2,1)S(1)}, u32[]{:S(2)}, u32[]{:S(2)}) collective-permute-start(bf16[128,1536]{1,0:T(8,128)(2,1)S(1)} %stack.15), channel_id=1, source_target_pairs={{0,16},{16,0},{32,48},{48,32},{64,80},{80,64},{96,112},{112,96},{1... | collective-permute-start | bytes 1179656 | tf_op jit(solution)/shard_map/ppermute | solution.py:224
  98.7 2.5 %collective-permute-start.17 = (bf16[64,1536]{1,0:T(8,128)(2,1)S(1)}, bf16[64,1536]{1,0:T(8,128)(2,1)S(1)}, u32[]{:S(2)}, u32[]{:S(2)}) collective-permute-start(bf16[64,1536]{1,0:T(8,128)(2,1)S(1)} %collective-permute-done.16.refs_1_), channel_id=1, source_target_pairs={{0,16},{16,0},{32,48},{48,32},{64,80},{80,64},{96,112},{112,96},{1... | collective-permute-start | bytes 589832 | tf_op jit(solution)/shard_map/ppermute | solution.py:224
  101.3 2.1 %collective-permute-start.8 = (bf16[64,1536]{1,0:T(8,128)(2,1)S(1)}, bf16[64,1536]{1,0:T(8,128)(2,1)S(1)}, u32[]{:S(2)}, u32[]{:S(2)}) collective-permute-start(bf16[64,1536]{1,0:T(8,128)(2,1)S(1)} %collective-permute-done.7.refs_1_), channel_id=1, source_target_pairs={{0,16},{16,0},{32,48},{48,32},{64,80},{80,64},{96,112},{112,96},{1... | collective-permute-start | bytes 589832 | tf_op jit(solution)/shard_map/ppermute | solution.py:224
  103.4 0.6 add_bitcast_fusion
  104.0 1.1 place.18
  105.1 1.1 place.19
  106.2 0.8 place.20
  107.0 1.1 place.21
  108.2 0.8 place.22
  109.0 1.1 place.23
  110.1 0.8 place.24
  111.0 1.1 place.25
  112.1 0.8 place.26
  113.0 1.1 place.27
  114.1 0.8 place.28
  114.9 1.1 place.29
  116.1 0.8 place.30
  116.9 0.9 place.31
  117.9 0.7 place.32
  118.6 0.9 place.33
  119.5 0.8 place.34
  120.4 0.7 place.35
  (107 shorter events, 3.4 us)
Async XLA Ops:
  0.6 1.9 %copy-start.7 = (f32[64]{0:T(128)S(1)}, f32[64]{0:T(128)}, u32[]{:S(2)}) copy-start(f32[64]{0:T(128)} %param.14) | copy-start | bytes 772
  0.7 1.9 %copy-start.8 = (f32[64]{0:T(128)S(1)}, f32[64]{0:T(128)}, u32[]{:S(2)}) copy-start(f32[64]{0:T(128)} %param.15) | copy-start | bytes 772
  0.7 1.9 %copy-start.5 = (f32[256,256]{1,0:T(8,128)S(1)}, f32[256,256]{1,0:T(8,128)}, u32[]{:S(2)}) copy-start(f32[256,256]{1,0:T(8,128)} %param.10) | copy-start | bytes 786436
  0.7 1.9 %copy-start.6 = (f32[256,256]{1,0:T(8,128)S(1)}, f32[256,256]{1,0:T(8,128)}, u32[]{:S(2)}) copy-start(f32[256,256]{1,0:T(8,128)} %param.11) | copy-start | bytes 786436
  0.7 1.9 %copy-start.3 = (f32[256,256]{1,0:T(8,128)S(1)}, f32[256,256]{1,0:T(8,128)}, u32[]{:S(2)}) copy-start(f32[256,256]{1,0:T(8,128)} %param.12) | copy-start | bytes 786436
  0.7 1.9 %copy-start.4 = (f32[256,256]{1,0:T(8,128)S(1)}, f32[256,256]{1,0:T(8,128)}, u32[]{:S(2)}) copy-start(f32[256,256]{1,0:T(8,128)} %param.13) | copy-start | bytes 786436
  2.6 20.4 %copy-start = (f32[256,1024]{1,0:T(8,128)}, f32[256,1024]{1,0:T(8,128)S(1)}, u32[]{:S(2)}) copy-start(f32[256,1024]{1,0:T(8,128)S(1)} %get-tuple-element.219.query) | copy-start | bytes 3145732
  2.7 20.3 %copy-start.1 = (f32[256,256]{1,0:T(8,128)}, f32[256,256]{1,0:T(8,128)S(1)}, u32[]{:S(2)}) copy-start(f32[256,256]{1,0:T(8,128)S(1)} %get-tuple-element.215.value) | copy-start | bytes 786436
  2.8 20.2 %copy-start.2 = (f32[256,256]{1,0:T(8,128)}, f32[256,256]{1,0:T(8,128)S(1)}, u32[]{:S(2)}) copy-start(f32[256,256]{1,0:T(8,128)S(1)} %get-tuple-element.221.key) | copy-start | bytes 786436
  3.7 18.6 %all-to-all-start = ((f32[16,1,1600]{2,1,0:T(1,128)}), f32[16,1,1600]{2,1,0:T(1,128)S(1)}, u32[]{:S(2)}, u32[]{:S(2)}) async-start(f32[16,1,1600]{2,1,0:T(1,128)} %broadcast_in_dim.17), calls=%async_computation | async-start | bytes 212992 | tf_op jit(solution)/shard_map/all_to_all | solution.py:199
  13.7 18.3 %collective-permute-start.18 = (f32[64,1536]{1,0:T(8,128)S(1)}, f32[64,1536]{1,0:T(8,128)S(1)}, u32[]{:S(2)}, u32[]{:S(2)}) collective-permute-start(f32[64,1536]{1,0:T(8,128)S(1)} %pack.1), channel_id=1, source_target_pairs={{0,32},{16,240},{32,64},{48,16},{64,96},{80,48},{96,128},{112,80},... | collective-permute-start | bytes 1179656 | tf_op jit(solution)/shard_map/ppermute | solution.py:185
  23.0 4.4 %collective-permute-start = (bf16[64,1536]{1,0:T(8,128)(2,1)S(1)}, bf16[64,1536]{1,0:T(8,128)(2,1)S(1)}, u32[]{:S(2)}, u32[]{:S(2)}) collective-permute-start(bf16[64,1536]{1,0:T(8,128)(2,1)S(1)} %get-tuple-element.112), channel_id=1, source_target_pairs={{0,16},{16,0},{32,48},{48,32},{64,80},{80,64},{96,112},{112,96},{1... | collective-permute-start | bytes 589832 | tf_op jit(solution)/shard_map/ppermute | solution.py:224
  23.1 5.1 %collective-permute-start.9 = (bf16[64,1536]{1,0:T(8,128)(2,1)S(1)}, bf16[64,1536]{1,0:T(8,128)(2,1)S(1)}, u32[]{:S(2)}, u32[]{:S(2)}) collective-permute-start(bf16[64,1536]{1,0:T(8,128)(2,1)S(1)} %get-tuple-element.113), channel_id=1, source_target_pairs={{0,16},{16,0},{32,48},{48,32},{64,80},{80,64},{96,112},{112,96},{1... | collective-permute-start | bytes 589832 | tf_op jit(solution)/shard_map/ppermute | solution.py:224
  23.6 2.5 %collective-permute-start.46 = (bf16[32,128]{1,0:T(8,128)(2,1)S(1)}, bf16[32,128]{1,0:T(8,128)(2,1)S(1)}, u32[]{:S(2)}, u32[]{:S(2)}) collective-permute-start(bf16[32,128]{1,0:T(8,128)(2,1)S(1)} %get-tuple-element.213), channel_id=1, source_target_pairs={{0,4},{4,0},{8,12},{12,8},{1,5},{5,1},{9,13},{13,9},{2,6},{6,2},{1... | collective-permute-start | bytes 24584 | tf_op jit(solution)/shard_map/ppermute | solution.py:283
  24.8 4.8 %collective-permute-start.25 = (bf16[64,1536]{1,0:T(8,128)(2,1)S(1)}, bf16[64,1536]{1,0:T(8,128)(2,1)S(1)}, u32[]{:S(2)}, u32[]{:S(2)}) collective-permute-start(bf16[64,1536]{1,0:T(8,128)(2,1)S(1)} %get-tuple-element.117), channel_id=1, source_target_pairs={{0,32},{16,240},{32,64},{48,16},{64,96},{80,48},{96,128},{112,80},... | collective-permute-start | bytes 589832 | tf_op jit(solution)/shard_map/ppermute | solution.py:230
  26.1 14.2 %collective-permute-start.45 = (bf16[128,1536]{1,0:T(8,128)(2,1)S(1)}, bf16[128,1536]{1,0:T(8,128)(2,1)S(1)}, u32[]{:S(2)}, u32[]{:S(2)}) collective-permute-start(bf16[128,1536]{1,0:T(8,128)(2,1)S(1)} %get-tuple-element.118.refs_0_), channel_id=1, source_target_pairs={{0,16},{16,0},{32,48},{48,32},{64,80},{80,64},{96,112},{112,96},{1... | collective-permute-start | bytes 1179656 | tf_op jit(solution)/shard_map/ppermute | solution.py:224
  27.4 7.2 %collective-permute-start.1 = (bf16[64,1536]{1,0:T(8,128)(2,1)S(1)}, bf16[64,1536]{1,0:T(8,128)(2,1)S(1)}, u32[]{:S(2)}, u32[]{:S(2)}) collective-permute-start(bf16[64,1536]{1,0:T(8,128)(2,1)S(1)} %collective-permute-done.refs_3_), channel_id=1, source_target_pairs={{0,32},{16,240},{32,64},{48,16},{64,96},{80,48},{96,128},{112,80},... | collective-permute-start | bytes 589832 | tf_op jit(solution)/shard_map/ppermute | solution.py:230
  28.2 9.2 %collective-permute-start.10 = (bf16[64,1536]{1,0:T(8,128)(2,1)S(1)}, bf16[64,1536]{1,0:T(8,128)(2,1)S(1)}, u32[]{:S(2)}, u32[]{:S(2)}) collective-permute-start(bf16[64,1536]{1,0:T(8,128)(2,1)S(1)} %collective-permute-done.9.refs_2_), channel_id=1, source_target_pairs={{0,32},{16,240},{32,64},{48,16},{64,96},{80,48},{96,128},{112,80},... | collective-permute-start | bytes 589832 | tf_op jit(solution)/shard_map/ppermute | solution.py:230
  29.6 4.0 %collective-permute-start.47 = (bf16[32,128]{1,0:T(8,128)(2,1)S(1)}, bf16[32,128]{1,0:T(8,128)(2,1)S(1)}, u32[]{:S(2)}, u32[]{:S(2)}) collective-permute-start(bf16[32,128]{1,0:T(8,128)(2,1)S(1)} %add.22), channel_id=1, source_target_pairs={{0,8},{4,12},{8,0},{12,4},{1,9},{5,13},{9,1},{13,5},{2,10},{6,14},... | collective-permute-start | bytes 24584 | tf_op jit(solution)/shard_map/ppermute | solution.py:283
  32.1 8.4 %collective-permute-start.26 = (bf16[64,1536]{1,0:T(8,128)(2,1)S(1)}, bf16[64,1536]{1,0:T(8,128)(2,1)S(1)}, u32[]{:S(2)}, u32[]{:S(2)}) collective-permute-start(bf16[64,1536]{1,0:T(8,128)(2,1)S(1)} %collective-permute-done.25.second.refs_2_), channel_id=1, source_target_pairs={{0,32},{16,240},{32,64},{48,16},{64,96},{80,48},{96,128},{112,80},... | collective-permute-start | bytes 589832 | tf_op jit(solution)/shard_map/ppermute | solution.py:230
  33.6 6.9 %collective-permute-start.19 = (bf16[64,1536]{1,0:T(8,128)(2,1)S(1)}, bf16[64,1536]{1,0:T(8,128)(2,1)S(1)}, u32[]{:S(2)}, u32[]{:S(2)}) collective-permute-start(bf16[64,1536]{1,0:T(8,128)(2,1)S(1)} %receive.1.first.refs_0_), channel_id=1, source_target_pairs={{0,32},{16,240},{32,64},{48,16},{64,96},{80,48},{96,128},{112,80},... | collective-permute-start | bytes 589832 | tf_op jit(solution)/shard_map/ppermute | solution.py:230
  34.6 15.7 %collective-permute-start.43 = (bf16[128,1536]{1,0:T(8,128)(2,1)S(1)}, bf16[128,1536]{1,0:T(8,128)(2,1)S(1)}, u32[]{:S(2)}, u32[]{:S(2)}) collective-permute-start(bf16[128,1536]{1,0:T(8,128)(2,1)S(1)} %stack.24), channel_id=1, source_target_pairs={{0,16},{16,0},{32,48},{48,32},{64,80},{80,64},{96,112},{112,96},{1... | collective-permute-start | bytes 1179656 | tf_op jit(solution)/shard_map/ppermute | solution.py:224
  37.4 5.6 %collective-permute-start.11 = (bf16[64,1536]{1,0:T(8,128)(2,1)S(1)}, bf16[64,1536]{1,0:T(8,128)(2,1)S(1)}, u32[]{:S(2)}, u32[]{:S(2)}) collective-permute-start(bf16[64,1536]{1,0:T(8,128)(2,1)S(1)} %collective-permute-done.10.first.refs_0_), channel_id=1, source_target_pairs={{0,32},{16,240},{32,64},{48,16},{64,96},{80,48},{96,128},{112,80},... | collective-permute-start | bytes 589832 | tf_op jit(solution)/shard_map/ppermute | solution.py:230
  40.4 13.7 %collective-permute-start.44 = (bf16[128,1536]{1,0:T(8,128)(2,1)S(1)}, bf16[128,1536]{1,0:T(8,128)(2,1)S(1)}, u32[]{:S(2)}, u32[]{:S(2)}) collective-permute-start(bf16[128,1536]{1,0:T(8,128)(2,1)S(1)} %stack.25), channel_id=1, source_target_pairs={{0,16},{16,0},{32,48},{48,32},{64,80},{80,64},{96,112},{112,96},{1... | collective-permute-start | bytes 1179656 | tf_op jit(solution)/shard_map/ppermute | solution.py:224
  40.5 5.6 %collective-permute-start.2 = (bf16[64,1536]{1,0:T(8,128)(2,1)S(1)}, bf16[64,1536]{1,0:T(8,128)(2,1)S(1)}, u32[]{:S(2)}, u32[]{:S(2)}) collective-permute-start(bf16[64,1536]{1,0:T(8,128)(2,1)S(1)} %collective-permute-done.1.second.refs_1_), channel_id=1, source_target_pairs={{0,32},{16,240},{32,64},{48,16},{64,96},{80,48},{96,128},{112,80},... | collective-permute-start | bytes 589832 | tf_op jit(solution)/shard_map/ppermute | solution.py:230
  40.6 8.0 %collective-permute-start.27 = (bf16[64,1536]{1,0:T(8,128)(2,1)S(1)}, bf16[64,1536]{1,0:T(8,128)(2,1)S(1)}, u32[]{:S(2)}, u32[]{:S(2)}) collective-permute-start(bf16[64,1536]{1,0:T(8,128)(2,1)S(1)} %collective-permute-done.26.second.refs_1_), channel_id=1, source_target_pairs={{0,32},{16,240},{32,64},{48,16},{64,96},{80,48},{96,128},{112,80},... | collective-permute-start | bytes 589832 | tf_op jit(solution)/shard_map/ppermute | solution.py:230
  42.9 8.2 %collective-permute-start.20 = (bf16[64,1536]{1,0:T(8,128)(2,1)S(1)}, bf16[64,1536]{1,0:T(8,128)(2,1)S(1)}, u32[]{:S(2)}, u32[]{:S(2)}) collective-permute-start(bf16[64,1536]{1,0:T(8,128)(2,1)S(1)} %collective-permute-done.19.first.refs_1_), channel_id=1, source_target_pairs={{0,32},{16,240},{32,64},{48,16},{64,96},{80,48},{96,128},{112,80},... | collective-permute-start | bytes 589832 | tf_op jit(solution)/shard_map/ppermute | solution.py:230
  46.1 15.9 %collective-permute-start.41 = (bf16[128,1536]{1,0:T(8,128)(2,1)S(1)}, bf16[128,1536]{1,0:T(8,128)(2,1)S(1)}, u32[]{:S(2)}, u32[]{:S(2)}) collective-permute-start(bf16[128,1536]{1,0:T(8,128)(2,1)S(1)} %stack.22), channel_id=1, source_target_pairs={{0,16},{16,0},{32,48},{48,32},{64,80},{80,64},{96,112},{112,96},{1... | collective-permute-start | bytes 1179656 | tf_op jit(solution)/shard_map/ppermute | solution.py:224
  48.6 5.6 %collective-permute-start.12 = (bf16[64,1536]{1,0:T(8,128)(2,1)S(1)}, bf16[64,1536]{1,0:T(8,128)(2,1)S(1)}, u32[]{:S(2)}, u32[]{:S(2)}) collective-permute-start(bf16[64,1536]{1,0:T(8,128)(2,1)S(1)} %collective-permute-done.11.first.refs_0_), channel_id=1, source_target_pairs={{0,32},{16,240},{32,64},{48,16},{64,96},{80,48},{96,128},{112,80},... | collective-permute-start | bytes 589832 | tf_op jit(solution)/shard_map/ppermute | solution.py:230
  50.3 14.9 %collective-permute-start.42 = (bf16[128,1536]{1,0:T(8,128)(2,1)S(1)}, bf16[128,1536]{1,0:T(8,128)(2,1)S(1)}, u32[]{:S(2)}, u32[]{:S(2)}) collective-permute-start(bf16[128,1536]{1,0:T(8,128)(2,1)S(1)} %stack.23), channel_id=1, source_target_pairs={{0,16},{16,0},{32,48},{48,32},{64,80},{80,64},{96,112},{112,96},{1... | collective-permute-start | bytes 1179656 | tf_op jit(solution)/shard_map/ppermute | solution.py:224
  51.1 5.6 %collective-permute-start.3 = (bf16[64,1536]{1,0:T(8,128)(2,1)S(1)}, bf16[64,1536]{1,0:T(8,128)(2,1)S(1)}, u32[]{:S(2)}, u32[]{:S(2)}) collective-permute-start(bf16[64,1536]{1,0:T(8,128)(2,1)S(1)} %collective-permute-done.2.second.refs_1_), channel_id=1, source_target_pairs={{0,32},{16,240},{32,64},{48,16},{64,96},{80,48},{96,128},{112,80},... | collective-permute-start | bytes 589832 | tf_op jit(solution)/shard_map/ppermute | solution.py:230
  54.1 5.9 %collective-permute-start.28 = (bf16[64,1536]{1,0:T(8,128)(2,1)S(1)}, bf16[64,1536]{1,0:T(8,128)(2,1)S(1)}, u32[]{:S(2)}, u32[]{:S(2)}) collective-permute-start(bf16[64,1536]{1,0:T(8,128)(2,1)S(1)} %collective-permute-done.27.second.refs_1_), channel_id=1, source_target_pairs={{0,32},{16,240},{32,64},{48,16},{64,96},{80,48},{96,128},{112,80},... | collective-permute-start | bytes 589832 | tf_op jit(solution)/shard_map/ppermute | solution.py:230
  54.2 8.1 %collective-permute-start.21 = (bf16[64,1536]{1,0:T(8,128)(2,1)S(1)}, bf16[64,1536]{1,0:T(8,128)(2,1)S(1)}, u32[]{:S(2)}, u32[]{:S(2)}) collective-permute-start(bf16[64,1536]{1,0:T(8,128)(2,1)S(1)} %collective-permute-done.20.first.refs_0_), channel_id=1, source_target_pairs={{0,32},{16,240},{32,64},{48,16},{64,96},{80,48},{96,128},{112,80},... | collective-permute-start | bytes 589832 | tf_op jit(solution)/shard_map/ppermute | solution.py:230
  56.7 16.4 %collective-permute-start.39 = (bf16[128,1536]{1,0:T(8,128)(2,1)S(1)}, bf16[128,1536]{1,0:T(8,128)(2,1)S(1)}, u32[]{:S(2)}, u32[]{:S(2)}) collective-permute-start(bf16[128,1536]{1,0:T(8,128)(2,1)S(1)} %stack.20), channel_id=1, source_target_pairs={{0,16},{16,0},{32,48},{48,32},{64,80},{80,64},{96,112},{112,96},{1... | collective-permute-start | bytes 1179656 | tf_op jit(solution)/shard_map/ppermute | solution.py:224
  60.0 5.3 %collective-permute-start.13 = (bf16[64,1536]{1,0:T(8,128)(2,1)S(1)}, bf16[64,1536]{1,0:T(8,128)(2,1)S(1)}, u32[]{:S(2)}, u32[]{:S(2)}) collective-permute-start(bf16[64,1536]{1,0:T(8,128)(2,1)S(1)} %collective-permute-done.12.first.refs_0_), channel_id=1, source_target_pairs={{0,32},{16,240},{32,64},{48,16},{64,96},{80,48},{96,128},{112,80},... | collective-permute-start | bytes 589832 | tf_op jit(solution)/shard_map/ppermute | solution.py:230
  62.0 14.9 %collective-permute-start.40 = (bf16[128,1536]{1,0:T(8,128)(2,1)S(1)}, bf16[128,1536]{1,0:T(8,128)(2,1)S(1)}, u32[]{:S(2)}, u32[]{:S(2)}) collective-permute-start(bf16[128,1536]{1,0:T(8,128)(2,1)S(1)} %stack.21), channel_id=1, source_target_pairs={{0,16},{16,0},{32,48},{48,32},{64,80},{80,64},{96,112},{112,96},{1... | collective-permute-start | bytes 1179656 | tf_op jit(solution)/shard_map/ppermute | solution.py:224
  62.2 5.6 %collective-permute-start.4 = (bf16[64,1536]{1,0:T(8,128)(2,1)S(1)}, bf16[64,1536]{1,0:T(8,128)(2,1)S(1)}, u32[]{:S(2)}, u32[]{:S(2)}) collective-permute-start(bf16[64,1536]{1,0:T(8,128)(2,1)S(1)} %collective-permute-done.3.second.refs_1_), channel_id=1, source_target_pairs={{0,32},{16,240},{32,64},{48,16},{64,96},{80,48},{96,128},{112,80},... | collective-permute-start | bytes 589832 | tf_op jit(solution)/shard_map/ppermute | solution.py:230
  65.2 6.5 %collective-permute-start.29 = (bf16[64,1536]{1,0:T(8,128)(2,1)S(1)}, bf16[64,1536]{1,0:T(8,128)(2,1)S(1)}, u32[]{:S(2)}, u32[]{:S(2)}) collective-permute-start(bf16[64,1536]{1,0:T(8,128)(2,1)S(1)} %collective-permute-done.28.second.refs_1_), channel_id=1, source_target_pairs={{0,32},{16,240},{32,64},{48,16},{64,96},{80,48},{96,128},{112,80},... | collective-permute-start | bytes 589832 | tf_op jit(solution)/shard_map/ppermute | solution.py:230
  65.3 8.6 %collective-permute-start.22 = (bf16[64,1536]{1,0:T(8,128)(2,1)S(1)}, bf16[64,1536]{1,0:T(8,128)(2,1)S(1)}, u32[]{:S(2)}, u32[]{:S(2)}) collective-permute-start(bf16[64,1536]{1,0:T(8,128)(2,1)S(1)} %collective-permute-done.21.first.refs_0_), channel_id=1, source_target_pairs={{0,32},{16,240},{32,64},{48,16},{64,96},{80,48},{96,128},{112,80},... | collective-permute-start | bytes 589832 | tf_op jit(solution)/shard_map/ppermute | solution.py:230
  67.8 16.9 %collective-permute-start.37 = (bf16[128,1536]{1,0:T(8,128)(2,1)S(1)}, bf16[128,1536]{1,0:T(8,128)(2,1)S(1)}, u32[]{:S(2)}, u32[]{:S(2)}) collective-permute-start(bf16[128,1536]{1,0:T(8,128)(2,1)S(1)} %stack.18), channel_id=1, source_target_pairs={{0,16},{16,0},{32,48},{48,32},{64,80},{80,64},{96,112},{112,96},{1... | collective-permute-start | bytes 1179656 | tf_op jit(solution)/shard_map/ppermute | solution.py:224
  71.6 5.3 %collective-permute-start.14 = (bf16[64,1536]{1,0:T(8,128)(2,1)S(1)}, bf16[64,1536]{1,0:T(8,128)(2,1)S(1)}, u32[]{:S(2)}, u32[]{:S(2)}) collective-permute-start(bf16[64,1536]{1,0:T(8,128)(2,1)S(1)} %collective-permute-done.13.first.refs_0_), channel_id=1, source_target_pairs={{0,32},{16,240},{32,64},{48,16},{64,96},{80,48},{96,128},{112,80},... | collective-permute-start | bytes 589832 | tf_op jit(solution)/shard_map/ppermute | solution.py:230
  73.0 14.9 %collective-permute-start.38 = (bf16[128,1536]{1,0:T(8,128)(2,1)S(1)}, bf16[128,1536]{1,0:T(8,128)(2,1)S(1)}, u32[]{:S(2)}, u32[]{:S(2)}) collective-permute-start(bf16[128,1536]{1,0:T(8,128)(2,1)S(1)} %stack.19), channel_id=1, source_target_pairs={{0,16},{16,0},{32,48},{48,32},{64,80},{80,64},{96,112},{112,96},{1... | collective-permute-start | bytes 1179656 | tf_op jit(solution)/shard_map/ppermute | solution.py:224
  73.9 5.6 %collective-permute-start.5 = (bf16[64,1536]{1,0:T(8,128)(2,1)S(1)}, bf16[64,1536]{1,0:T(8,128)(2,1)S(1)}, u32[]{:S(2)}, u32[]{:S(2)}) collective-permute-start(bf16[64,1536]{1,0:T(8,128)(2,1)S(1)} %collective-permute-done.4.second.refs_1_), channel_id=1, source_target_pairs={{0,32},{16,240},{32,64},{48,16},{64,96},{80,48},{96,128},{112,80},... | collective-permute-start | bytes 589832 | tf_op jit(solution)/shard_map/ppermute | solution.py:230
  76.8 5.9 %collective-permute-start.30 = (bf16[64,1536]{1,0:T(8,128)(2,1)S(1)}, bf16[64,1536]{1,0:T(8,128)(2,1)S(1)}, u32[]{:S(2)}, u32[]{:S(2)}) collective-permute-start(bf16[64,1536]{1,0:T(8,128)(2,1)S(1)} %collective-permute-done.29.second.refs_1_), channel_id=1, source_target_pairs={{0,32},{16,240},{32,64},{48,16},{64,96},{80,48},{96,128},{112,80},... | collective-permute-start | bytes 589832 | tf_op jit(solution)/shard_map/ppermute | solution.py:230
  76.9 8.1 %collective-permute-start.23 = (bf16[64,1536]{1,0:T(8,128)(2,1)S(1)}, bf16[64,1536]{1,0:T(8,128)(2,1)S(1)}, u32[]{:S(2)}, u32[]{:S(2)}) collective-permute-start(bf16[64,1536]{1,0:T(8,128)(2,1)S(1)} %collective-permute-done.22.first.refs_0_), channel_id=1, source_target_pairs={{0,32},{16,240},{32,64},{48,16},{64,96},{80,48},{96,128},{112,80},... | collective-permute-start | bytes 589832 | tf_op jit(solution)/shard_map/ppermute | solution.py:230
  79.4 16.4 %collective-permute-start.35 = (bf16[128,1536]{1,0:T(8,128)(2,1)S(1)}, bf16[128,1536]{1,0:T(8,128)(2,1)S(1)}, u32[]{:S(2)}, u32[]{:S(2)}) collective-permute-start(bf16[128,1536]{1,0:T(8,128)(2,1)S(1)} %stack.16), channel_id=1, source_target_pairs={{0,16},{16,0},{32,48},{48,32},{64,80},{80,64},{96,112},{112,96},{1... | collective-permute-start | bytes 1179656 | tf_op jit(solution)/shard_map/ppermute | solution.py:224
  82.7 5.3 %collective-permute-start.15 = (bf16[64,1536]{1,0:T(8,128)(2,1)S(1)}, bf16[64,1536]{1,0:T(8,128)(2,1)S(1)}, u32[]{:S(2)}, u32[]{:S(2)}) collective-permute-start(bf16[64,1536]{1,0:T(8,128)(2,1)S(1)} %collective-permute-done.14.first.refs_0_), channel_id=1, source_target_pairs={{0,32},{16,240},{32,64},{48,16},{64,96},{80,48},{96,128},{112,80},... | collective-permute-start | bytes 589832 | tf_op jit(solution)/shard_map/ppermute | solution.py:230
  84.7 13.9 %collective-permute-start.36 = (bf16[128,1536]{1,0:T(8,128)(2,1)S(1)}, bf16[128,1536]{1,0:T(8,128)(2,1)S(1)}, u32[]{:S(2)}, u32[]{:S(2)}) collective-permute-start(bf16[128,1536]{1,0:T(8,128)(2,1)S(1)} %stack.17), channel_id=1, source_target_pairs={{0,16},{16,0},{32,48},{48,32},{64,80},{80,64},{96,112},{112,96},{1... | collective-permute-start | bytes 1179656 | tf_op jit(solution)/shard_map/ppermute | solution.py:224
  85.0 5.6 %collective-permute-start.6 = (bf16[64,1536]{1,0:T(8,128)(2,1)S(1)}, bf16[64,1536]{1,0:T(8,128)(2,1)S(1)}, u32[]{:S(2)}, u32[]{:S(2)}) collective-permute-start(bf16[64,1536]{1,0:T(8,128)(2,1)S(1)} %collective-permute-done.5.second.refs_1_), channel_id=1, source_target_pairs={{0,32},{16,240},{32,64},{48,16},{64,96},{80,48},{96,128},{112,80},... | collective-permute-start | bytes 589832 | tf_op jit(solution)/shard_map/ppermute | solution.py:230
  87.9 5.7 %collective-permute-start.31 = (bf16[64,1536]{1,0:T(8,128)(2,1)S(1)}, bf16[64,1536]{1,0:T(8,128)(2,1)S(1)}, u32[]{:S(2)}, u32[]{:S(2)}) collective-permute-start(bf16[64,1536]{1,0:T(8,128)(2,1)S(1)} %collective-permute-done.30.second.refs_1_), channel_id=1, source_target_pairs={{0,32},{16,240},{32,64},{48,16},{64,96},{80,48},{96,128},{112,80},... | collective-permute-start | bytes 589832 | tf_op jit(solution)/shard_map/ppermute | solution.py:230
  88.0 8.6 %collective-permute-start.24 = (bf16[64,1536]{1,0:T(8,128)(2,1)S(1)}, bf16[64,1536]{1,0:T(8,128)(2,1)S(1)}, u32[]{:S(2)}, u32[]{:S(2)}) collective-permute-start(bf16[64,1536]{1,0:T(8,128)(2,1)S(1)} %collective-permute-done.23.first.refs_0_), channel_id=1, source_target_pairs={{0,32},{16,240},{32,64},{48,16},{64,96},{80,48},{96,128},{112,80},... | collective-permute-start | bytes 589832 | tf_op jit(solution)/shard_map/ppermute | solution.py:230
  90.5 8.2 %collective-permute-start.16 = (bf16[64,1536]{1,0:T(8,128)(2,1)S(1)}, bf16[64,1536]{1,0:T(8,128)(2,1)S(1)}, u32[]{:S(2)}, u32[]{:S(2)}) collective-permute-start(bf16[64,1536]{1,0:T(8,128)(2,1)S(1)} %collective-permute-done.15.first.refs_0_), channel_id=1, source_target_pairs={{0,32},{16,240},{32,64},{48,16},{64,96},{80,48},{96,128},{112,80},... | collective-permute-start | bytes 589832 | tf_op jit(solution)/shard_map/ppermute | solution.py:230
  93.7 7.6 %collective-permute-start.7 = (bf16[64,1536]{1,0:T(8,128)(2,1)S(1)}, bf16[64,1536]{1,0:T(8,128)(2,1)S(1)}, u32[]{:S(2)}, u32[]{:S(2)}) collective-permute-start(bf16[64,1536]{1,0:T(8,128)(2,1)S(1)} %collective-permute-done.6.second.refs_1_), channel_id=1, source_target_pairs={{0,32},{16,240},{32,64},{48,16},{64,96},{80,48},{96,128},{112,80},... | collective-permute-start | bytes 589832 | tf_op jit(solution)/shard_map/ppermute | solution.py:230
  95.8 21.1 %collective-permute-start.33 = (bf16[128,1536]{1,0:T(8,128)(2,1)S(1)}, bf16[128,1536]{1,0:T(8,128)(2,1)S(1)}, u32[]{:S(2)}, u32[]{:S(2)}) collective-permute-start(bf16[128,1536]{1,0:T(8,128)(2,1)S(1)} %stack.14), channel_id=1, source_target_pairs={{0,16},{16,0},{32,48},{48,32},{64,80},{80,64},{96,112},{112,96},{1... | collective-permute-start | bytes 1179656 | tf_op jit(solution)/shard_map/ppermute | solution.py:224
  96.7 20.3 %collective-permute-start.34 = (bf16[128,1536]{1,0:T(8,128)(2,1)S(1)}, bf16[128,1536]{1,0:T(8,128)(2,1)S(1)}, u32[]{:S(2)}, u32[]{:S(2)}) collective-permute-start(bf16[128,1536]{1,0:T(8,128)(2,1)S(1)} %stack.15), channel_id=1, source_target_pairs={{0,16},{16,0},{32,48},{48,32},{64,80},{80,64},{96,112},{112,96},{1... | collective-permute-start | bytes 1179656 | tf_op jit(solution)/shard_map/ppermute | solution.py:224
  98.6 20.0 %collective-permute-start.32 = (bf16[128,1536]{1,0:T(8,128)(2,1)S(1)}, bf16[128,1536]{1,0:T(8,128)(2,1)S(1)}, u32[]{:S(2)}, u32[]{:S(2)}) collective-permute-start(bf16[128,1536]{1,0:T(8,128)(2,1)S(1)} %stack.13), channel_id=1, source_target_pairs={{0,16},{16,0},{32,48},{48,32},{64,80},{80,64},{96,112},{112,96},{1... | collective-permute-start | bytes 1179656 | tf_op jit(solution)/shard_map/ppermute | solution.py:224
  98.7 20.8 %collective-permute-start.17 = (bf16[64,1536]{1,0:T(8,128)(2,1)S(1)}, bf16[64,1536]{1,0:T(8,128)(2,1)S(1)}, u32[]{:S(2)}, u32[]{:S(2)}) collective-permute-start(bf16[64,1536]{1,0:T(8,128)(2,1)S(1)} %collective-permute-done.16.refs_1_), channel_id=1, source_target_pairs={{0,16},{16,0},{32,48},{48,32},{64,80},{80,64},{96,112},{112,96},{1... | collective-permute-start | bytes 589832 | tf_op jit(solution)/shard_map/ppermute | solution.py:224
  101.3 19.1 %collective-permute-start.8 = (bf16[64,1536]{1,0:T(8,128)(2,1)S(1)}, bf16[64,1536]{1,0:T(8,128)(2,1)S(1)}, u32[]{:S(2)}, u32[]{:S(2)}) collective-permute-start(bf16[64,1536]{1,0:T(8,128)(2,1)S(1)} %collective-permute-done.7.refs_1_), channel_id=1, source_target_pairs={{0,16},{16,0},{32,48},{48,32},{64,80},{80,64},{96,112},{112,96},{1... | collective-permute-start | bytes 589832 | tf_op jit(solution)/shard_map/ppermute | solution.py:224

commit v2 on v1

--- a/solution.py
+++ b/solution.py
@@ -254,18 +254,19 @@
         [],
         [mine("a", 1), mine("a", 2), mine("b", 1), (hands["hand0"], (0, True, True, 0))],
         [],
-        [mine("c", 1), mine("d", 1)],
+        [],
     ]
     for hop in range(2, LAST):
         puts += [
             [],
-            [mine("a", hop + 1), mine("b", hop), theirs("near", hop - 1), theirs("far", hop - 1)],
+            [mine(*p) for p in (("a", hop + 1), ("b", hop), ("c", hop - 1), ("d", hop - 1))]
+            + [theirs(kind, hop - 1) for kind in ("near", "far")],
             [],
-            [mine("c", hop), mine("d", hop)],
+            [],
         ]
     puts += [
-        [theirs("near", LAST - 1), theirs("far", LAST - 1)],
-        [mine("b", LAST)],
+        [mine(*p) for p in (("b", LAST), ("c", LAST - 1), ("d", LAST - 1))]
+        + [theirs(kind, LAST - 1) for kind in ("near", "far")],
         [theirs("near", LAST), mine("c", LAST)],
         [(hands[f"c{LAST}"], (LAST, True, False, 0)), mine("d", LAST)],
         [(hands[f"d{LAST}"], (LAST, True, False, 1))],

time: 121 us -> 117 us (0.967)
  Pallas kernels: 17.9 us -> 13.5 us
    pallas_call x18 -> x11, Pallas kernels: 16.8 us -> 12.4 us  [placed(): pl.pallas_call(functools.partial(place, spots), out_shape=shapes, in_spec...]
  transfers between devices with their start and end apart: 49 -> 49, of which waited for: 9 -> 9; matrix products, arithmetic and copies ran while one was open for 1% -> 1% of each run, Pallas kernels for 14% -> 11%
where the time goes in v2:
time: 117 us
  starting transfers between devices  86.8 us (74%)
  Pallas kernels  13.5 us (12%)
  waiting for transfers between devices  11.6 us (10%)
  other arithmetic  2.58 us (2%)
  between operations  1.44 us (1%)
    ppermute x27, starting transfers between devices, body(): have[kind, hop] = lax.ppermute(have[kind, hop - 1], 'zero', both_ways())  43.3 us
    ppermute x18, starting transfers between devices, swap(): return lax.ppermute(piece, 'zero', other_core())  27.2 us
    pallas_call x11, Pallas kernels, placed(): pl.pallas_call(functools.partial(place, spots), out_shape=shapes, in_spec...  12.4 us
    all_to_all x1, starting transfers between devices, body(): lax.all_to_all(copies, 'zero', split_axis=0, concat_axis=0, tiled=True)  9.97 us
    all_to_all x1, waiting for transfers between devices, body(): lax.all_to_all(copies, 'zero', split_axis=0, concat_axis=0, tiled=True)  5.96 us
    ppermute x27, waiting for transfers between devices, body(): have[kind, hop] = lax.ppermute(have[kind, hop - 1], 'zero', both_ways())  3.66 us
    ppermute x2, starting transfers between devices, body(): theirs = lax.ppermute(serve_norm, 'tp', [(i, i ^ k) for i in range(tp)])  3.66 us
    ppermute x1, starting transfers between devices, body(): early = lax.ppermute(early, 'zero', both_ways())  2.65 us
  transfers between devices with their start and end apart: 49, of which 9 were waited for; matrix products, arithmetic and copies ran while one was open for 1% of the time, Pallas kernels for 11%

profile of v2, /device:TPU:1, one launch (start us, length us, event | category | flops | bytes accessed | tf_op | source)
XLA Modules:
  0.0 116.9 jit_solution(17752131318552370761)
XLA Ops:
  0.7 1.8 %multiply_reduce_fusion = (f32[1024]{0:T(1024)S(1)}, f32[256,1024]{1,0:T(8,128)S(1)}) fusion(f32[256,1024]{1,0:T(8,128)} %param.8, f32[256,1024]{1,0:T(8,128)} %param.9), kind=kLoop, calls=%fused_computation | loop fusion | flops 1309696 | bytes 3149824 | tf_op jit(solution)/shard_map/reduce_sum | solution.py:187
  2.6 0.1 multiply_reduce_fusion.1
  2.8 0.9 broadcast_in_dim.17
  3.7 10.0 %all-to-all-start = ((f32[16,1,1600]{2,1,0:T(1,128)}), f32[16,1,1600]{2,1,0:T(1,128)S(1)}, u32[]{:S(2)}, u32[]{:S(2)}) async-start(f32[16,1,1600]{2,1,0:T(1,128)} %broadcast_in_dim.17), calls=%async_computation | async-start | bytes 212992 | tf_op jit(solution)/shard_map/all_to_all | solution.py:199
  13.7 2.6 %collective-permute-start.18 = (f32[64,1536]{1,0:T(8,128)S(1)}, f32[64,1536]{1,0:T(8,128)S(1)}, u32[]{:S(2)}, u32[]{:S(2)}) collective-permute-start(f32[64,1536]{1,0:T(8,128)S(1)} %pack.1), channel_id=1, source_target_pairs={{0,32},{16,240},{32,64},{48,16},{64,96},{80,48},{96,128},{112,80},... | collective-permute-start | bytes 1179656 | tf_op jit(solution)/shard_map/ppermute | solution.py:185
  16.4 6.0 %all-to-all-done = f32[16,1,1600]{2,1,0:T(1,128)S(1)} async-done(((f32[16,1,1600]{2,1,0:T(1,128)}), f32[16,1,1600]{2,1,0:T(1,128)S(1)}, u32[]{:S(2)}, u32[]{:S(2)}) %all-to-all-start) | async-done | bytes 102432 | tf_op jit(solution)/shard_map/all_to_all | solution.py:199
  22.3 0.6 normalise.1
  23.1 0.5 collective-permute-start.9
  23.6 1.2 %collective-permute-start.46 = (bf16[32,128]{1,0:T(8,128)(2,1)S(1)}, bf16[32,128]{1,0:T(8,128)(2,1)S(1)}, u32[]{:S(2)}, u32[]{:S(2)}) collective-permute-start(bf16[32,128]{1,0:T(8,128)(2,1)S(1)} %get-tuple-element.207), channel_id=1, source_target_pairs={{0,4},{4,0},{8,12},{12,8},{1,5},{5,1},{9,13},{13,9},{2,6},{6,2},{1... | collective-permute-start | bytes 24584 | tf_op jit(solution)/shard_map/ppermute | solution.py:284
  24.8 1.3 %collective-permute-done.46 = bf16[32,128]{1,0:T(8,128)(2,1)S(1)} collective-permute-done((bf16[32,128]{1,0:T(8,128)(2,1)S(1)}, bf16[32,128]{1,0:T(8,128)(2,1)S(1)}, u32[]{:S(2)}, u32[]{:S(2)}) %collective-permute-start.46) | collective-permute-done | bytes 8224 | tf_op jit(solution)/shard_map/ppermute | solution.py:284
  26.1 1.2 %collective-permute-start.45 = (bf16[128,1536]{1,0:T(8,128)(2,1)S(1)}, bf16[128,1536]{1,0:T(8,128)(2,1)S(1)}, u32[]{:S(2)}, u32[]{:S(2)}) collective-permute-start(bf16[128,1536]{1,0:T(8,128)(2,1)S(1)} %get-tuple-element.115.refs_0_), channel_id=1, source_target_pairs={{0,16},{16,0},{32,48},{48,32},{64,80},{80,64},{96,112},{112,96},{1... | collective-permute-start | bytes 1179656 | tf_op jit(solution)/shard_map/ppermute | solution.py:224
  27.4 0.8 collective-permute-start.1
  28.2 1.4 %collective-permute-done.25.second.refs_2_ = bf16[64,1536]{1,0:T(8,128)(2,1)S(1)} collective-permute-done((bf16[64,1536]{1,0:T(8,128)(2,1)S(1)}, bf16[64,1536]{1,0:T(8,128)(2,1)S(1)}, u32[]{:S(2)}, u32[]{:S(2)}) %collective-permute-start.25) | collective-permute-done | bytes 196640 | tf_op jit(solution)/shard_map/ppermute | solution.py:230
  29.6 2.5 %collective-permute-start.47 = (bf16[32,128]{1,0:T(8,128)(2,1)S(1)}, bf16[32,128]{1,0:T(8,128)(2,1)S(1)}, u32[]{:S(2)}, u32[]{:S(2)}) collective-permute-start(bf16[32,128]{1,0:T(8,128)(2,1)S(1)} %add.22), channel_id=1, source_target_pairs={{0,8},{4,12},{8,0},{12,4},{1,9},{5,13},{9,1},{13,5},{2,10},{6,14},... | collective-permute-start | bytes 24584 | tf_op jit(solution)/shard_map/ppermute | solution.py:284
  32.1 0.9 collective-permute-start.26
  33.0 0.6 collective-permute-done.47
  33.6 0.9 collective-permute-start.19
  34.6 2.8 %collective-permute-start.43 = (bf16[128,1536]{1,0:T(8,128)(2,1)S(1)}, bf16[128,1536]{1,0:T(8,128)(2,1)S(1)}, u32[]{:S(2)}, u32[]{:S(2)}) collective-permute-start(bf16[128,1536]{1,0:T(8,128)(2,1)S(1)} %stack.24), channel_id=1, source_target_pairs={{0,16},{16,0},{32,48},{48,32},{64,80},{80,64},{96,112},{112,96},{1... | collective-permute-start | bytes 1179656 | tf_op jit(solution)/shard_map/ppermute | solution.py:224
  37.4 3.0 %collective-permute-start.11 = (bf16[64,1536]{1,0:T(8,128)(2,1)S(1)}, bf16[64,1536]{1,0:T(8,128)(2,1)S(1)}, u32[]{:S(2)}, u32[]{:S(2)}) collective-permute-start(bf16[64,1536]{1,0:T(8,128)(2,1)S(1)} %collective-permute-done.10.first.refs_2_), channel_id=1, source_target_pairs={{0,32},{16,240},{32,64},{48,16},{64,96},{80,48},{96,128},{112,80},... | collective-permute-start | bytes 589832 | tf_op jit(solution)/shard_map/ppermute | solution.py:230
  40.6 1.7 %collective-permute-start.27 = (bf16[64,1536]{1,0:T(8,128)(2,1)S(1)}, bf16[64,1536]{1,0:T(8,128)(2,1)S(1)}, u32[]{:S(2)}, u32[]{:S(2)}) collective-permute-start(bf16[64,1536]{1,0:T(8,128)(2,1)S(1)} %collective-permute-done.26.second.refs_1_), channel_id=1, source_target_pairs={{0,32},{16,240},{32,64},{48,16},{64,96},{80,48},{96,128},{112,80},... | collective-permute-start | bytes 589832 | tf_op jit(solution)/shard_map/ppermute | solution.py:230
  42.3 0.6 collective-permute-done.11.first.refs_2_
  42.9 3.1 %collective-permute-start.20 = (bf16[64,1536]{1,0:T(8,128)(2,1)S(1)}, bf16[64,1536]{1,0:T(8,128)(2,1)S(1)}, u32[]{:S(2)}, u32[]{:S(2)}) collective-permute-start(bf16[64,1536]{1,0:T(8,128)(2,1)S(1)} %collective-permute-done.19.first.refs_1_), channel_id=1, source_target_pairs={{0,32},{16,240},{32,64},{48,16},{64,96},{80,48},{96,128},{112,80},... | collective-permute-start | bytes 589832 | tf_op jit(solution)/shard_map/ppermute | solution.py:230
  46.1 2.5 %collective-permute-start.41 = (bf16[128,1536]{1,0:T(8,128)(2,1)S(1)}, bf16[128,1536]{1,0:T(8,128)(2,1)S(1)}, u32[]{:S(2)}, u32[]{:S(2)}) collective-permute-start(bf16[128,1536]{1,0:T(8,128)(2,1)S(1)} %stack.22), channel_id=1, source_target_pairs={{0,16},{16,0},{32,48},{48,32},{64,80},{80,64},{96,112},{112,96},{1... | collective-permute-start | bytes 1179656 | tf_op jit(solution)/shard_map/ppermute | solution.py:224
  48.6 1.7 %collective-permute-start.12 = (bf16[64,1536]{1,0:T(8,128)(2,1)S(1)}, bf16[64,1536]{1,0:T(8,128)(2,1)S(1)}, u32[]{:S(2)}, u32[]{:S(2)}) collective-permute-start(bf16[64,1536]{1,0:T(8,128)(2,1)S(1)} %collective-permute-done.11.first.refs_2_), channel_id=1, source_target_pairs={{0,32},{16,240},{32,64},{48,16},{64,96},{80,48},{96,128},{112,80},... | collective-permute-start | bytes 589832 | tf_op jit(solution)/shard_map/ppermute | solution.py:230
  50.3 0.8 collective-permute-start.42
  51.1 3.0 %collective-permute-start.3 = (bf16[64,1536]{1,0:T(8,128)(2,1)S(1)}, bf16[64,1536]{1,0:T(8,128)(2,1)S(1)}, u32[]{:S(2)}, u32[]{:S(2)}) collective-permute-start(bf16[64,1536]{1,0:T(8,128)(2,1)S(1)} %collective-permute-done.2.second.refs_3_), channel_id=1, source_target_pairs={{0,32},{16,240},{32,64},{48,16},{64,96},{80,48},{96,128},{112,80},... | collective-permute-start | bytes 589832 | tf_op jit(solution)/shard_map/ppermute | solution.py:230
  54.2 1.8 %collective-permute-start.21 = (bf16[64,1536]{1,0:T(8,128)(2,1)S(1)}, bf16[64,1536]{1,0:T(8,128)(2,1)S(1)}, u32[]{:S(2)}, u32[]{:S(2)}) collective-permute-start(bf16[64,1536]{1,0:T(8,128)(2,1)S(1)} %collective-permute-done.20.first.refs_0_), channel_id=1, source_target_pairs={{0,32},{16,240},{32,64},{48,16},{64,96},{80,48},{96,128},{112,80},... | collective-permute-start | bytes 589832 | tf_op jit(solution)/shard_map/ppermute | solution.py:230
  56.0 0.7 collective-permute-done.3.second.refs_3_
  56.7 3.3 %collective-permute-start.39 = (bf16[128,1536]{1,0:T(8,128)(2,1)S(1)}, bf16[128,1536]{1,0:T(8,128)(2,1)S(1)}, u32[]{:S(2)}, u32[]{:S(2)}) collective-permute-start(bf16[128,1536]{1,0:T(8,128)(2,1)S(1)} %stack.20), channel_id=1, source_target_pairs={{0,16},{16,0},{32,48},{48,32},{64,80},{80,64},{96,112},{112,96},{1... | collective-permute-start | bytes 1179656 | tf_op jit(solution)/shard_map/ppermute | solution.py:224
  60.0 1.9 %collective-permute-start.13 = (bf16[64,1536]{1,0:T(8,128)(2,1)S(1)}, bf16[64,1536]{1,0:T(8,128)(2,1)S(1)}, u32[]{:S(2)}, u32[]{:S(2)}) collective-permute-start(bf16[64,1536]{1,0:T(8,128)(2,1)S(1)} %collective-permute-done.12.first.refs_2_), channel_id=1, source_target_pairs={{0,32},{16,240},{32,64},{48,16},{64,96},{80,48},{96,128},{112,80},... | collective-permute-start | bytes 589832 | tf_op jit(solution)/shard_map/ppermute | solution.py:230
  62.0 0.3 collective-permute-start.40
  62.2 3.0 %collective-permute-start.4 = (bf16[64,1536]{1,0:T(8,128)(2,1)S(1)}, bf16[64,1536]{1,0:T(8,128)(2,1)S(1)}, u32[]{:S(2)}, u32[]{:S(2)}) collective-permute-start(bf16[64,1536]{1,0:T(8,128)(2,1)S(1)} %collective-permute-done.3.second.refs_3_), channel_id=1, source_target_pairs={{0,32},{16,240},{32,64},{48,16},{64,96},{80,48},{96,128},{112,80},... | collective-permute-start | bytes 589832 | tf_op jit(solution)/shard_map/ppermute | solution.py:230
  65.3 2.4 %collective-permute-start.22 = (bf16[64,1536]{1,0:T(8,128)(2,1)S(1)}, bf16[64,1536]{1,0:T(8,128)(2,1)S(1)}, u32[]{:S(2)}, u32[]{:S(2)}) collective-permute-start(bf16[64,1536]{1,0:T(8,128)(2,1)S(1)} %collective-permute-done.21.first.refs_0_), channel_id=1, source_target_pairs={{0,32},{16,240},{32,64},{48,16},{64,96},{80,48},{96,128},{112,80},... | collective-permute-start | bytes 589832 | tf_op jit(solution)/shard_map/ppermute | solution.py:230
  67.7 0.1 collective-permute-done.4.second.refs_3_
  67.8 3.8 %collective-permute-start.37 = (bf16[128,1536]{1,0:T(8,128)(2,1)S(1)}, bf16[128,1536]{1,0:T(8,128)(2,1)S(1)}, u32[]{:S(2)}, u32[]{:S(2)}) collective-permute-start(bf16[128,1536]{1,0:T(8,128)(2,1)S(1)} %stack.18), channel_id=1, source_target_pairs={{0,16},{16,0},{32,48},{48,32},{64,80},{80,64},{96,112},{112,96},{1... | collective-permute-start | bytes 1179656 | tf_op jit(solution)/shard_map/ppermute | solution.py:224
  71.6 1.4 %collective-permute-start.14 = (bf16[64,1536]{1,0:T(8,128)(2,1)S(1)}, bf16[64,1536]{1,0:T(8,128)(2,1)S(1)}, u32[]{:S(2)}, u32[]{:S(2)}) collective-permute-start(bf16[64,1536]{1,0:T(8,128)(2,1)S(1)} %collective-permute-done.13.first.refs_2_), channel_id=1, source_target_pairs={{0,32},{16,240},{32,64},{48,16},{64,96},{80,48},{96,128},{112,80},... | collective-permute-start | bytes 589832 | tf_op jit(solution)/shard_map/ppermute | solution.py:230
  73.0 0.8 collective-permute-start.38
  73.9 3.0 %collective-permute-start.5 = (bf16[64,1536]{1,0:T(8,128)(2,1)S(1)}, bf16[64,1536]{1,0:T(8,128)(2,1)S(1)}, u32[]{:S(2)}, u32[]{:S(2)}) collective-permute-start(bf16[64,1536]{1,0:T(8,128)(2,1)S(1)} %collective-permute-done.4.second.refs_3_), channel_id=1, source_target_pairs={{0,32},{16,240},{32,64},{48,16},{64,96},{80,48},{96,128},{112,80},... | collective-permute-start | bytes 589832 | tf_op jit(solution)/shard_map/ppermute | solution.py:230
  76.9 1.8 %collective-permute-start.23 = (bf16[64,1536]{1,0:T(8,128)(2,1)S(1)}, bf16[64,1536]{1,0:T(8,128)(2,1)S(1)}, u32[]{:S(2)}, u32[]{:S(2)}) collective-permute-start(bf16[64,1536]{1,0:T(8,128)(2,1)S(1)} %collective-permute-done.22.first.refs_0_), channel_id=1, source_target_pairs={{0,32},{16,240},{32,64},{48,16},{64,96},{80,48},{96,128},{112,80},... | collective-permute-start | bytes 589832 | tf_op jit(solution)/shard_map/ppermute | solution.py:230
  78.8 0.7 collective-permute-done.5.second.refs_3_
  79.4 3.3 %collective-permute-start.35 = (bf16[128,1536]{1,0:T(8,128)(2,1)S(1)}, bf16[128,1536]{1,0:T(8,128)(2,1)S(1)}, u32[]{:S(2)}, u32[]{:S(2)}) collective-permute-start(bf16[128,1536]{1,0:T(8,128)(2,1)S(1)} %stack.16), channel_id=1, source_target_pairs={{0,16},{16,0},{32,48},{48,32},{64,80},{80,64},{96,112},{112,96},{1... | collective-permute-start | bytes 1179656 | tf_op jit(solution)/shard_map/ppermute | solution.py:224
  82.7 1.9 %collective-permute-start.15 = (bf16[64,1536]{1,0:T(8,128)(2,1)S(1)}, bf16[64,1536]{1,0:T(8,128)(2,1)S(1)}, u32[]{:S(2)}, u32[]{:S(2)}) collective-permute-start(bf16[64,1536]{1,0:T(8,128)(2,1)S(1)} %collective-permute-done.14.first.refs_2_), channel_id=1, source_target_pairs={{0,32},{16,240},{32,64},{48,16},{64,96},{80,48},{96,128},{112,80},... | collective-permute-start | bytes 589832 | tf_op jit(solution)/shard_map/ppermute | solution.py:230
  84.7 0.3 collective-permute-start.36
  85.0 3.0 %collective-permute-start.6 = (bf16[64,1536]{1,0:T(8,128)(2,1)S(1)}, bf16[64,1536]{1,0:T(8,128)(2,1)S(1)}, u32[]{:S(2)}, u32[]{:S(2)}) collective-permute-start(bf16[64,1536]{1,0:T(8,128)(2,1)S(1)} %collective-permute-done.5.second.refs_3_), channel_id=1, source_target_pairs={{0,32},{16,240},{32,64},{48,16},{64,96},{80,48},{96,128},{112,80},... | collective-permute-start | bytes 589832 | tf_op jit(solution)/shard_map/ppermute | solution.py:230
  88.0 2.4 %collective-permute-start.24 = (bf16[64,1536]{1,0:T(8,128)(2,1)S(1)}, bf16[64,1536]{1,0:T(8,128)(2,1)S(1)}, u32[]{:S(2)}, u32[]{:S(2)}) collective-permute-start(bf16[64,1536]{1,0:T(8,128)(2,1)S(1)} %collective-permute-done.23.first.refs_0_), channel_id=1, source_target_pairs={{0,32},{16,240},{32,64},{48,16},{64,96},{80,48},{96,128},{112,80},... | collective-permute-start | bytes 589832 | tf_op jit(solution)/shard_map/ppermute | solution.py:230
  90.4 0.1 collective-permute-done.6.second.refs_2_
  90.5 3.1 %collective-permute-start.16 = (bf16[64,1536]{1,0:T(8,128)(2,1)S(1)}, bf16[64,1536]{1,0:T(8,128)(2,1)S(1)}, u32[]{:S(2)}, u32[]{:S(2)}) collective-permute-start(bf16[64,1536]{1,0:T(8,128)(2,1)S(1)} %collective-permute-done.15.first.refs_1_), channel_id=1, source_target_pairs={{0,32},{16,240},{32,64},{48,16},{64,96},{80,48},{96,128},{112,80},... | collective-permute-start | bytes 589832 | tf_op jit(solution)/shard_map/ppermute | solution.py:230
  93.7 2.1 %collective-permute-start.7 = (bf16[64,1536]{1,0:T(8,128)(2,1)S(1)}, bf16[64,1536]{1,0:T(8,128)(2,1)S(1)}, u32[]{:S(2)}, u32[]{:S(2)}) collective-permute-start(bf16[64,1536]{1,0:T(8,128)(2,1)S(1)} %collective-permute-done.6.second.refs_2_), channel_id=1, source_target_pairs={{0,32},{16,240},{32,64},{48,16},{64,96},{80,48},{96,128},{112,80},... | collective-permute-start | bytes 589832 | tf_op jit(solution)/shard_map/ppermute | solution.py:230
  95.8 0.8 collective-permute-start.33
  96.7 1.9 %collective-permute-start.34 = (bf16[128,1536]{1,0:T(8,128)(2,1)S(1)}, bf16[128,1536]{1,0:T(8,128)(2,1)S(1)}, u32[]{:S(2)}, u32[]{:S(2)}) collective-permute-start(bf16[128,1536]{1,0:T(8,128)(2,1)S(1)} %stack.15), channel_id=1, source_target_pairs={{0,16},{16,0},{32,48},{48,32},{64,80},{80,64},{96,112},{112,96},{1... | collective-permute-start | bytes 1179656 | tf_op jit(solution)/shard_map/ppermute | solution.py:224
  98.7 2.5 %collective-permute-start.17 = (bf16[64,1536]{1,0:T(8,128)(2,1)S(1)}, bf16[64,1536]{1,0:T(8,128)(2,1)S(1)}, u32[]{:S(2)}, u32[]{:S(2)}) collective-permute-start(bf16[64,1536]{1,0:T(8,128)(2,1)S(1)} %collective-permute-done.16.refs_1_), channel_id=1, source_target_pairs={{0,16},{16,0},{32,48},{48,32},{64,80},{80,64},{96,112},{112,96},{1... | collective-permute-start | bytes 589832 | tf_op jit(solution)/shard_map/ppermute | solution.py:224
  101.3 2.1 %collective-permute-start.8 = (bf16[64,1536]{1,0:T(8,128)(2,1)S(1)}, bf16[64,1536]{1,0:T(8,128)(2,1)S(1)}, u32[]{:S(2)}, u32[]{:S(2)}) collective-permute-start(bf16[64,1536]{1,0:T(8,128)(2,1)S(1)} %collective-permute-done.7.refs_1_), channel_id=1, source_target_pairs={{0,16},{16,0},{32,48},{48,32},{64,80},{80,64},{96,112},{112,96},{1... | collective-permute-start | bytes 589832 | tf_op jit(solution)/shard_map/ppermute | solution.py:224
  103.4 0.6 add_bitcast_fusion
  104.0 1.1 place.11
  105.1 1.1 place.12
  106.2 1.3 %place.13 = (bf16[4096,1024]{1,0:T(8,128)(2,1)}, bf16[4096,256]{1,0:T(8,128)(2,1)}, bf16[4096,256]{1,0:T(8,128)(2,1)}) custom-call(bf16[64,1536]{1,0:T(8,128)(2,1)S(1)} %collective-permute-done.20.first.refs_0_, bf16[64,1536]{1,0:T(8,128)(2,1)S(1)} %collective-permute-done.26.second.refs_1_, ...), custom_call_target="tpu_custom_call", output_to_operand_aliasing={{0}: (6, {}), {1}: (7, {}), {2}: (8, {})} | custom-call | bytes 3145728 | tf_op jit(solution)/shard_map/place/pallas_call | solution.py:153
  107.6 1.3 %place.14 = (bf16[4096,1024]{1,0:T(8,128)(2,1)}, bf16[4096,256]{1,0:T(8,128)(2,1)}, bf16[4096,256]{1,0:T(8,128)(2,1)}) custom-call(bf16[64,1536]{1,0:T(8,128)(2,1)S(1)} %collective-permute-done.21.first.refs_0_, bf16[64,1536]{1,0:T(8,128)(2,1)S(1)} %collective-permute-done.27.second.refs_1_, ...), custom_call_target="tpu_custom_call", output_to_operand_aliasing={{0}: (6, {}), {1}: (7, {}), {2}: (8, {})} | custom-call | bytes 3145728 | tf_op jit(solution)/shard_map/place/pallas_call | solution.py:153
  108.9 1.3 %place.15 = (bf16[4096,1024]{1,0:T(8,128)(2,1)}, bf16[4096,256]{1,0:T(8,128)(2,1)}, bf16[4096,256]{1,0:T(8,128)(2,1)}) custom-call(bf16[64,1536]{1,0:T(8,128)(2,1)S(1)} %collective-permute-done.22.first.refs_0_, bf16[64,1536]{1,0:T(8,128)(2,1)S(1)} %collective-permute-done.28.second.refs_1_, ...), custom_call_target="tpu_custom_call", output_to_operand_aliasing={{0}: (6, {}), {1}: (7, {}), {2}: (8, {})} | custom-call | bytes 3145728 | tf_op jit(solution)/shard_map/place/pallas_call | solution.py:153
  110.3 1.3 %place.16 = (bf16[4096,1024]{1,0:T(8,128)(2,1)}, bf16[4096,256]{1,0:T(8,128)(2,1)}, bf16[4096,256]{1,0:T(8,128)(2,1)}) custom-call(bf16[64,1536]{1,0:T(8,128)(2,1)S(1)} %collective-permute-done.23.first.refs_0_, bf16[64,1536]{1,0:T(8,128)(2,1)S(1)} %collective-permute-done.29.second.refs_1_, ...), custom_call_target="tpu_custom_call", output_to_operand_aliasing={{0}: (6, {}), {1}: (7, {}), {2}: (8, {})} | custom-call | bytes 3145728 | tf_op jit(solution)/shard_map/place/pallas_call | solution.py:153
  111.6 1.3 %place.17 = (bf16[4096,1024]{1,0:T(8,128)(2,1)}, bf16[4096,256]{1,0:T(8,128)(2,1)}, bf16[4096,256]{1,0:T(8,128)(2,1)}) custom-call(bf16[64,1536]{1,0:T(8,128)(2,1)S(1)} %collective-permute-done.24.first.refs_0_, bf16[64,1536]{1,0:T(8,128)(2,1)S(1)} %collective-permute-done.30.second.refs_1_, ...), custom_call_target="tpu_custom_call", output_to_operand_aliasing={{0}: (6, {}), {1}: (7, {}), {2}: (8, {})} | custom-call | bytes 3145728 | tf_op jit(solution)/shard_map/place/pallas_call | solution.py:153
  113.0 1.2 %place.18 = (bf16[4096,1024]{1,0:T(8,128)(2,1)}, bf16[4096,256]{1,0:T(8,128)(2,1)}, bf16[4096,256]{1,0:T(8,128)(2,1)}) custom-call(bf16[64,1536]{1,0:T(8,128)(2,1)S(1)} %collective-permute-done.31.second.refs_0_, bf16[64,1536]{1,0:T(8,128)(2,1)S(1)} %collective-permute-done.15.first.refs_1_, ...), custom_call_target="tpu_custom_call", output_to_operand_aliasing={{0}: (5, {}), {1}: (6, {}), {2}: (7, {})} | custom-call | bytes 2752512 | tf_op jit(solution)/shard_map/place/pallas_call | solution.py:153
  114.2 0.9 place.19
  115.1 0.8 place.20
  116.0 0.7 place.21
  (106 shorter events, 1.5 us)
Async XLA Ops:
  0.6 1.9 %copy-start.7 = (f32[64]{0:T(128)S(1)}, f32[64]{0:T(128)}, u32[]{:S(2)}) copy-start(f32[64]{0:T(128)} %param.14) | copy-start | bytes 772
  0.7 1.9 %copy-start.8 = (f32[64]{0:T(128)S(1)}, f32[64]{0:T(128)}, u32[]{:S(2)}) copy-start(f32[64]{0:T(128)} %param.15) | copy-start | bytes 772
  0.7 1.9 %copy-start.5 = (f32[256,256]{1,0:T(8,128)S(1)}, f32[256,256]{1,0:T(8,128)}, u32[]{:S(2)}) copy-start(f32[256,256]{1,0:T(8,128)} %param.10) | copy-start | bytes 786436
  0.7 1.9 %copy-start.6 = (f32[256,256]{1,0:T(8,128)S(1)}, f32[256,256]{1,0:T(8,128)}, u32[]{:S(2)}) copy-start(f32[256,256]{1,0:T(8,128)} %param.11) | copy-start | bytes 786436
  0.7 1.9 %copy-start.3 = (f32[256,256]{1,0:T(8,128)S(1)}, f32[256,256]{1,0:T(8,128)}, u32[]{:S(2)}) copy-start(f32[256,256]{1,0:T(8,128)} %param.12) | copy-start | bytes 786436
  0.7 1.9 %copy-start.4 = (f32[256,256]{1,0:T(8,128)S(1)}, f32[256,256]{1,0:T(8,128)}, u32[]{:S(2)}) copy-start(f32[256,256]{1,0:T(8,128)} %param.13) | copy-start | bytes 786436
  2.6 20.4 %copy-start = (f32[256,1024]{1,0:T(8,128)}, f32[256,1024]{1,0:T(8,128)S(1)}, u32[]{:S(2)}) copy-start(f32[256,1024]{1,0:T(8,128)S(1)} %get-tuple-element.213.query) | copy-start | bytes 3145732
  2.7 20.3 %copy-start.1 = (f32[256,256]{1,0:T(8,128)}, f32[256,256]{1,0:T(8,128)S(1)}, u32[]{:S(2)}) copy-start(f32[256,256]{1,0:T(8,128)S(1)} %get-tuple-element.209.value) | copy-start | bytes 786436
  2.8 20.2 %copy-start.2 = (f32[256,256]{1,0:T(8,128)}, f32[256,256]{1,0:T(8,128)S(1)}, u32[]{:S(2)}) copy-start(f32[256,256]{1,0:T(8,128)S(1)} %get-tuple-element.215.key) | copy-start | bytes 786436
  3.7 18.6 %all-to-all-start = ((f32[16,1,1600]{2,1,0:T(1,128)}), f32[16,1,1600]{2,1,0:T(1,128)S(1)}, u32[]{:S(2)}, u32[]{:S(2)}) async-start(f32[16,1,1600]{2,1,0:T(1,128)} %broadcast_in_dim.17), calls=%async_computation | async-start | bytes 212992 | tf_op jit(solution)/shard_map/all_to_all | solution.py:199
  13.7 18.3 %collective-permute-start.18 = (f32[64,1536]{1,0:T(8,128)S(1)}, f32[64,1536]{1,0:T(8,128)S(1)}, u32[]{:S(2)}, u32[]{:S(2)}) collective-permute-start(f32[64,1536]{1,0:T(8,128)S(1)} %pack.1), channel_id=1, source_target_pairs={{0,32},{16,240},{32,64},{48,16},{64,96},{80,48},{96,128},{112,80},... | collective-permute-start | bytes 1179656 | tf_op jit(solution)/shard_map/ppermute | solution.py:185
  23.0 4.4 %collective-permute-start = (bf16[64,1536]{1,0:T(8,128)(2,1)S(1)}, bf16[64,1536]{1,0:T(8,128)(2,1)S(1)}, u32[]{:S(2)}, u32[]{:S(2)}) collective-permute-start(bf16[64,1536]{1,0:T(8,128)(2,1)S(1)} %get-tuple-element.109), channel_id=1, source_target_pairs={{0,16},{16,0},{32,48},{48,32},{64,80},{80,64},{96,112},{112,96},{1... | collective-permute-start | bytes 589832 | tf_op jit(solution)/shard_map/ppermute | solution.py:224
  23.1 5.1 %collective-permute-start.9 = (bf16[64,1536]{1,0:T(8,128)(2,1)S(1)}, bf16[64,1536]{1,0:T(8,128)(2,1)S(1)}, u32[]{:S(2)}, u32[]{:S(2)}) collective-permute-start(bf16[64,1536]{1,0:T(8,128)(2,1)S(1)} %get-tuple-element.110), channel_id=1, source_target_pairs={{0,16},{16,0},{32,48},{48,32},{64,80},{80,64},{96,112},{112,96},{1... | collective-permute-start | bytes 589832 | tf_op jit(solution)/shard_map/ppermute | solution.py:224
  23.6 2.5 %collective-permute-start.46 = (bf16[32,128]{1,0:T(8,128)(2,1)S(1)}, bf16[32,128]{1,0:T(8,128)(2,1)S(1)}, u32[]{:S(2)}, u32[]{:S(2)}) collective-permute-start(bf16[32,128]{1,0:T(8,128)(2,1)S(1)} %get-tuple-element.207), channel_id=1, source_target_pairs={{0,4},{4,0},{8,12},{12,8},{1,5},{5,1},{9,13},{13,9},{2,6},{6,2},{1... | collective-permute-start | bytes 24584 | tf_op jit(solution)/shard_map/ppermute | solution.py:284
  24.8 4.8 %collective-permute-start.25 = (bf16[64,1536]{1,0:T(8,128)(2,1)S(1)}, bf16[64,1536]{1,0:T(8,128)(2,1)S(1)}, u32[]{:S(2)}, u32[]{:S(2)}) collective-permute-start(bf16[64,1536]{1,0:T(8,128)(2,1)S(1)} %get-tuple-element.114), channel_id=1, source_target_pairs={{0,32},{16,240},{32,64},{48,16},{64,96},{80,48},{96,128},{112,80},... | collective-permute-start | bytes 589832 | tf_op jit(solution)/shard_map/ppermute | solution.py:230
  26.1 14.2 %collective-permute-start.45 = (bf16[128,1536]{1,0:T(8,128)(2,1)S(1)}, bf16[128,1536]{1,0:T(8,128)(2,1)S(1)}, u32[]{:S(2)}, u32[]{:S(2)}) collective-permute-start(bf16[128,1536]{1,0:T(8,128)(2,1)S(1)} %get-tuple-element.115.refs_0_), channel_id=1, source_target_pairs={{0,16},{16,0},{32,48},{48,32},{64,80},{80,64},{96,112},{112,96},{1... | collective-permute-start | bytes 1179656 | tf_op jit(solution)/shard_map/ppermute | solution.py:224
  27.4 7.2 %collective-permute-start.1 = (bf16[64,1536]{1,0:T(8,128)(2,1)S(1)}, bf16[64,1536]{1,0:T(8,128)(2,1)S(1)}, u32[]{:S(2)}, u32[]{:S(2)}) collective-permute-start(bf16[64,1536]{1,0:T(8,128)(2,1)S(1)} %collective-permute-done.refs_3_), channel_id=1, source_target_pairs={{0,32},{16,240},{32,64},{48,16},{64,96},{80,48},{96,128},{112,80},... | collective-permute-start | bytes 589832 | tf_op jit(solution)/shard_map/ppermute | solution.py:230
  28.2 9.2 %collective-permute-start.10 = (bf16[64,1536]{1,0:T(8,128)(2,1)S(1)}, bf16[64,1536]{1,0:T(8,128)(2,1)S(1)}, u32[]{:S(2)}, u32[]{:S(2)}) collective-permute-start(bf16[64,1536]{1,0:T(8,128)(2,1)S(1)} %collective-permute-done.9.refs_2_), channel_id=1, source_target_pairs={{0,32},{16,240},{32,64},{48,16},{64,96},{80,48},{96,128},{112,80},... | collective-permute-start | bytes 589832 | tf_op jit(solution)/shard_map/ppermute | solution.py:230
  29.6 4.0 %collective-permute-start.47 = (bf16[32,128]{1,0:T(8,128)(2,1)S(1)}, bf16[32,128]{1,0:T(8,128)(2,1)S(1)}, u32[]{:S(2)}, u32[]{:S(2)}) collective-permute-start(bf16[32,128]{1,0:T(8,128)(2,1)S(1)} %add.22), channel_id=1, source_target_pairs={{0,8},{4,12},{8,0},{12,4},{1,9},{5,13},{9,1},{13,5},{2,10},{6,14},... | collective-permute-start | bytes 24584 | tf_op jit(solution)/shard_map/ppermute | solution.py:284
  32.1 8.4 %collective-permute-start.26 = (bf16[64,1536]{1,0:T(8,128)(2,1)S(1)}, bf16[64,1536]{1,0:T(8,128)(2,1)S(1)}, u32[]{:S(2)}, u32[]{:S(2)}) collective-permute-start(bf16[64,1536]{1,0:T(8,128)(2,1)S(1)} %collective-permute-done.25.second.refs_2_), channel_id=1, source_target_pairs={{0,32},{16,240},{32,64},{48,16},{64,96},{80,48},{96,128},{112,80},... | collective-permute-start | bytes 589832 | tf_op jit(solution)/shard_map/ppermute | solution.py:230
  33.6 6.9 %collective-permute-start.19 = (bf16[64,1536]{1,0:T(8,128)(2,1)S(1)}, bf16[64,1536]{1,0:T(8,128)(2,1)S(1)}, u32[]{:S(2)}, u32[]{:S(2)}) collective-permute-start(bf16[64,1536]{1,0:T(8,128)(2,1)S(1)} %receive.1.first.refs_0_), channel_id=1, source_target_pairs={{0,32},{16,240},{32,64},{48,16},{64,96},{80,48},{96,128},{112,80},... | collective-permute-start | bytes 589832 | tf_op jit(solution)/shard_map/ppermute | solution.py:230
  34.6 15.7 %collective-permute-start.43 = (bf16[128,1536]{1,0:T(8,128)(2,1)S(1)}, bf16[128,1536]{1,0:T(8,128)(2,1)S(1)}, u32[]{:S(2)}, u32[]{:S(2)}) collective-permute-start(bf16[128,1536]{1,0:T(8,128)(2,1)S(1)} %stack.24), channel_id=1, source_target_pairs={{0,16},{16,0},{32,48},{48,32},{64,80},{80,64},{96,112},{112,96},{1... | collective-permute-start | bytes 1179656 | tf_op jit(solution)/shard_map/ppermute | solution.py:224
  37.4 5.6 %collective-permute-start.11 = (bf16[64,1536]{1,0:T(8,128)(2,1)S(1)}, bf16[64,1536]{1,0:T(8,128)(2,1)S(1)}, u32[]{:S(2)}, u32[]{:S(2)}) collective-permute-start(bf16[64,1536]{1,0:T(8,128)(2,1)S(1)} %collective-permute-done.10.first.refs_2_), channel_id=1, source_target_pairs={{0,32},{16,240},{32,64},{48,16},{64,96},{80,48},{96,128},{112,80},... | collective-permute-start | bytes 589832 | tf_op jit(solution)/shard_map/ppermute | solution.py:230
  40.4 13.7 %collective-permute-start.44 = (bf16[128,1536]{1,0:T(8,128)(2,1)S(1)}, bf16[128,1536]{1,0:T(8,128)(2,1)S(1)}, u32[]{:S(2)}, u32[]{:S(2)}) collective-permute-start(bf16[128,1536]{1,0:T(8,128)(2,1)S(1)} %stack.25), channel_id=1, source_target_pairs={{0,16},{16,0},{32,48},{48,32},{64,80},{80,64},{96,112},{112,96},{1... | collective-permute-start | bytes 1179656 | tf_op jit(solution)/shard_map/ppermute | solution.py:224
  40.5 5.6 %collective-permute-start.2 = (bf16[64,1536]{1,0:T(8,128)(2,1)S(1)}, bf16[64,1536]{1,0:T(8,128)(2,1)S(1)}, u32[]{:S(2)}, u32[]{:S(2)}) collective-permute-start(bf16[64,1536]{1,0:T(8,128)(2,1)S(1)} %collective-permute-done.1.second.refs_3_), channel_id=1, source_target_pairs={{0,32},{16,240},{32,64},{48,16},{64,96},{80,48},{96,128},{112,80},... | collective-permute-start | bytes 589832 | tf_op jit(solution)/shard_map/ppermute | solution.py:230
  40.6 8.0 %collective-permute-start.27 = (bf16[64,1536]{1,0:T(8,128)(2,1)S(1)}, bf16[64,1536]{1,0:T(8,128)(2,1)S(1)}, u32[]{:S(2)}, u32[]{:S(2)}) collective-permute-start(bf16[64,1536]{1,0:T(8,128)(2,1)S(1)} %collective-permute-done.26.second.refs_1_), channel_id=1, source_target_pairs={{0,32},{16,240},{32,64},{48,16},{64,96},{80,48},{96,128},{112,80},... | collective-permute-start | bytes 589832 | tf_op jit(solution)/shard_map/ppermute | solution.py:230
  42.9 8.2 %collective-permute-start.20 = (bf16[64,1536]{1,0:T(8,128)(2,1)S(1)}, bf16[64,1536]{1,0:T(8,128)(2,1)S(1)}, u32[]{:S(2)}, u32[]{:S(2)}) collective-permute-start(bf16[64,1536]{1,0:T(8,128)(2,1)S(1)} %collective-permute-done.19.first.refs_1_), channel_id=1, source_target_pairs={{0,32},{16,240},{32,64},{48,16},{64,96},{80,48},{96,128},{112,80},... | collective-permute-start | bytes 589832 | tf_op jit(solution)/shard_map/ppermute | solution.py:230
  46.1 15.9 %collective-permute-start.41 = (bf16[128,1536]{1,0:T(8,128)(2,1)S(1)}, bf16[128,1536]{1,0:T(8,128)(2,1)S(1)}, u32[]{:S(2)}, u32[]{:S(2)}) collective-permute-start(bf16[128,1536]{1,0:T(8,128)(2,1)S(1)} %stack.22), channel_id=1, source_target_pairs={{0,16},{16,0},{32,48},{48,32},{64,80},{80,64},{96,112},{112,96},{1... | collective-permute-start | bytes 1179656 | tf_op jit(solution)/shard_map/ppermute | solution.py:224
  48.6 5.6 %collective-permute-start.12 = (bf16[64,1536]{1,0:T(8,128)(2,1)S(1)}, bf16[64,1536]{1,0:T(8,128)(2,1)S(1)}, u32[]{:S(2)}, u32[]{:S(2)}) collective-permute-start(bf16[64,1536]{1,0:T(8,128)(2,1)S(1)} %collective-permute-done.11.first.refs_2_), channel_id=1, source_target_pairs={{0,32},{16,240},{32,64},{48,16},{64,96},{80,48},{96,128},{112,80},... | collective-permute-start | bytes 589832 | tf_op jit(solution)/shard_map/ppermute | solution.py:230
  50.3 14.9 %collective-permute-start.42 = (bf16[128,1536]{1,0:T(8,128)(2,1)S(1)}, bf16[128,1536]{1,0:T(8,128)(2,1)S(1)}, u32[]{:S(2)}, u32[]{:S(2)}) collective-permute-start(bf16[128,1536]{1,0:T(8,128)(2,1)S(1)} %stack.23), channel_id=1, source_target_pairs={{0,16},{16,0},{32,48},{48,32},{64,80},{80,64},{96,112},{112,96},{1... | collective-permute-start | bytes 1179656 | tf_op jit(solution)/shard_map/ppermute | solution.py:224
  51.1 5.6 %collective-permute-start.3 = (bf16[64,1536]{1,0:T(8,128)(2,1)S(1)}, bf16[64,1536]{1,0:T(8,128)(2,1)S(1)}, u32[]{:S(2)}, u32[]{:S(2)}) collective-permute-start(bf16[64,1536]{1,0:T(8,128)(2,1)S(1)} %collective-permute-done.2.second.refs_3_), channel_id=1, source_target_pairs={{0,32},{16,240},{32,64},{48,16},{64,96},{80,48},{96,128},{112,80},... | collective-permute-start | bytes 589832 | tf_op jit(solution)/shard_map/ppermute | solution.py:230
  54.1 5.9 %collective-permute-start.28 = (bf16[64,1536]{1,0:T(8,128)(2,1)S(1)}, bf16[64,1536]{1,0:T(8,128)(2,1)S(1)}, u32[]{:S(2)}, u32[]{:S(2)}) collective-permute-start(bf16[64,1536]{1,0:T(8,128)(2,1)S(1)} %collective-permute-done.27.second.refs_1_), channel_id=1, source_target_pairs={{0,32},{16,240},{32,64},{48,16},{64,96},{80,48},{96,128},{112,80},... | collective-permute-start | bytes 589832 | tf_op jit(solution)/shard_map/ppermute | solution.py:230
  54.2 8.1 %collective-permute-start.21 = (bf16[64,1536]{1,0:T(8,128)(2,1)S(1)}, bf16[64,1536]{1,0:T(8,128)(2,1)S(1)}, u32[]{:S(2)}, u32[]{:S(2)}) collective-permute-start(bf16[64,1536]{1,0:T(8,128)(2,1)S(1)} %collective-permute-done.20.first.refs_0_), channel_id=1, source_target_pairs={{0,32},{16,240},{32,64},{48,16},{64,96},{80,48},{96,128},{112,80},... | collective-permute-start | bytes 589832 | tf_op jit(solution)/shard_map/ppermute | solution.py:230
  56.7 16.4 %collective-permute-start.39 = (bf16[128,1536]{1,0:T(8,128)(2,1)S(1)}, bf16[128,1536]{1,0:T(8,128)(2,1)S(1)}, u32[]{:S(2)}, u32[]{:S(2)}) collective-permute-start(bf16[128,1536]{1,0:T(8,128)(2,1)S(1)} %stack.20), channel_id=1, source_target_pairs={{0,16},{16,0},{32,48},{48,32},{64,80},{80,64},{96,112},{112,96},{1... | collective-permute-start | bytes 1179656 | tf_op jit(solution)/shard_map/ppermute | solution.py:224
  60.0 5.3 %collective-permute-start.13 = (bf16[64,1536]{1,0:T(8,128)(2,1)S(1)}, bf16[64,1536]{1,0:T(8,128)(2,1)S(1)}, u32[]{:S(2)}, u32[]{:S(2)}) collective-permute-start(bf16[64,1536]{1,0:T(8,128)(2,1)S(1)} %collective-permute-done.12.first.refs_2_), channel_id=1, source_target_pairs={{0,32},{16,240},{32,64},{48,16},{64,96},{80,48},{96,128},{112,80},... | collective-permute-start | bytes 589832 | tf_op jit(solution)/shard_map/ppermute | solution.py:230
  62.0 14.9 %collective-permute-start.40 = (bf16[128,1536]{1,0:T(8,128)(2,1)S(1)}, bf16[128,1536]{1,0:T(8,128)(2,1)S(1)}, u32[]{:S(2)}, u32[]{:S(2)}) collective-permute-start(bf16[128,1536]{1,0:T(8,128)(2,1)S(1)} %stack.21), channel_id=1, source_target_pairs={{0,16},{16,0},{32,48},{48,32},{64,80},{80,64},{96,112},{112,96},{1... | collective-permute-start | bytes 1179656 | tf_op jit(solution)/shard_map/ppermute | solution.py:224
  62.2 5.6 %collective-permute-start.4 = (bf16[64,1536]{1,0:T(8,128)(2,1)S(1)}, bf16[64,1536]{1,0:T(8,128)(2,1)S(1)}, u32[]{:S(2)}, u32[]{:S(2)}) collective-permute-start(bf16[64,1536]{1,0:T(8,128)(2,1)S(1)} %collective-permute-done.3.second.refs_3_), channel_id=1, source_target_pairs={{0,32},{16,240},{32,64},{48,16},{64,96},{80,48},{96,128},{112,80},... | collective-permute-start | bytes 589832 | tf_op jit(solution)/shard_map/ppermute | solution.py:230
  65.2 6.5 %collective-permute-start.29 = (bf16[64,1536]{1,0:T(8,128)(2,1)S(1)}, bf16[64,1536]{1,0:T(8,128)(2,1)S(1)}, u32[]{:S(2)}, u32[]{:S(2)}) collective-permute-start(bf16[64,1536]{1,0:T(8,128)(2,1)S(1)} %collective-permute-done.28.second.refs_1_), channel_id=1, source_target_pairs={{0,32},{16,240},{32,64},{48,16},{64,96},{80,48},{96,128},{112,80},... | collective-permute-start | bytes 589832 | tf_op jit(solution)/shard_map/ppermute | solution.py:230
  65.3 8.6 %collective-permute-start.22 = (bf16[64,1536]{1,0:T(8,128)(2,1)S(1)}, bf16[64,1536]{1,0:T(8,128)(2,1)S(1)}, u32[]{:S(2)}, u32[]{:S(2)}) collective-permute-start(bf16[64,1536]{1,0:T(8,128)(2,1)S(1)} %collective-permute-done.21.first.refs_0_), channel_id=1, source_target_pairs={{0,32},{16,240},{32,64},{48,16},{64,96},{80,48},{96,128},{112,80},... | collective-permute-start | bytes 589832 | tf_op jit(solution)/shard_map/ppermute | solution.py:230
  67.8 16.9 %collective-permute-start.37 = (bf16[128,1536]{1,0:T(8,128)(2,1)S(1)}, bf16[128,1536]{1,0:T(8,128)(2,1)S(1)}, u32[]{:S(2)}, u32[]{:S(2)}) collective-permute-start(bf16[128,1536]{1,0:T(8,128)(2,1)S(1)} %stack.18), channel_id=1, source_target_pairs={{0,16},{16,0},{32,48},{48,32},{64,80},{80,64},{96,112},{112,96},{1... | collective-permute-start | bytes 1179656 | tf_op jit(solution)/shard_map/ppermute | solution.py:224
  71.6 5.3 %collective-permute-start.14 = (bf16[64,1536]{1,0:T(8,128)(2,1)S(1)}, bf16[64,1536]{1,0:T(8,128)(2,1)S(1)}, u32[]{:S(2)}, u32[]{:S(2)}) collective-permute-start(bf16[64,1536]{1,0:T(8,128)(2,1)S(1)} %collective-permute-done.13.first.refs_2_), channel_id=1, source_target_pairs={{0,32},{16,240},{32,64},{48,16},{64,96},{80,48},{96,128},{112,80},... | collective-permute-start | bytes 589832 | tf_op jit(solution)/shard_map/ppermute | solution.py:230
  73.0 14.9 %collective-permute-start.38 = (bf16[128,1536]{1,0:T(8,128)(2,1)S(1)}, bf16[128,1536]{1,0:T(8,128)(2,1)S(1)}, u32[]{:S(2)}, u32[]{:S(2)}) collective-permute-start(bf16[128,1536]{1,0:T(8,128)(2,1)S(1)} %stack.19), channel_id=1, source_target_pairs={{0,16},{16,0},{32,48},{48,32},{64,80},{80,64},{96,112},{112,96},{1... | collective-permute-start | bytes 1179656 | tf_op jit(solution)/shard_map/ppermute | solution.py:224
  73.9 5.6 %collective-permute-start.5 = (bf16[64,1536]{1,0:T(8,128)(2,1)S(1)}, bf16[64,1536]{1,0:T(8,128)(2,1)S(1)}, u32[]{:S(2)}, u32[]{:S(2)}) collective-permute-start(bf16[64,1536]{1,0:T(8,128)(2,1)S(1)} %collective-permute-done.4.second.refs_3_), channel_id=1, source_target_pairs={{0,32},{16,240},{32,64},{48,16},{64,96},{80,48},{96,128},{112,80},... | collective-permute-start | bytes 589832 | tf_op jit(solution)/shard_map/ppermute | solution.py:230
  76.8 5.9 %collective-permute-start.30 = (bf16[64,1536]{1,0:T(8,128)(2,1)S(1)}, bf16[64,1536]{1,0:T(8,128)(2,1)S(1)}, u32[]{:S(2)}, u32[]{:S(2)}) collective-permute-start(bf16[64,1536]{1,0:T(8,128)(2,1)S(1)} %collective-permute-done.29.second.refs_1_), channel_id=1, source_target_pairs={{0,32},{16,240},{32,64},{48,16},{64,96},{80,48},{96,128},{112,80},... | collective-permute-start | bytes 589832 | tf_op jit(solution)/shard_map/ppermute | solution.py:230
  76.9 8.1 %collective-permute-start.23 = (bf16[64,1536]{1,0:T(8,128)(2,1)S(1)}, bf16[64,1536]{1,0:T(8,128)(2,1)S(1)}, u32[]{:S(2)}, u32[]{:S(2)}) collective-permute-start(bf16[64,1536]{1,0:T(8,128)(2,1)S(1)} %collective-permute-done.22.first.refs_0_), channel_id=1, source_target_pairs={{0,32},{16,240},{32,64},{48,16},{64,96},{80,48},{96,128},{112,80},... | collective-permute-start | bytes 589832 | tf_op jit(solution)/shard_map/ppermute | solution.py:230
  79.4 16.4 %collective-permute-start.35 = (bf16[128,1536]{1,0:T(8,128)(2,1)S(1)}, bf16[128,1536]{1,0:T(8,128)(2,1)S(1)}, u32[]{:S(2)}, u32[]{:S(2)}) collective-permute-start(bf16[128,1536]{1,0:T(8,128)(2,1)S(1)} %stack.16), channel_id=1, source_target_pairs={{0,16},{16,0},{32,48},{48,32},{64,80},{80,64},{96,112},{112,96},{1... | collective-permute-start | bytes 1179656 | tf_op jit(solution)/shard_map/ppermute | solution.py:224
  82.7 5.3 %collective-permute-start.15 = (bf16[64,1536]{1,0:T(8,128)(2,1)S(1)}, bf16[64,1536]{1,0:T(8,128)(2,1)S(1)}, u32[]{:S(2)}, u32[]{:S(2)}) collective-permute-start(bf16[64,1536]{1,0:T(8,128)(2,1)S(1)} %collective-permute-done.14.first.refs_2_), channel_id=1, source_target_pairs={{0,32},{16,240},{32,64},{48,16},{64,96},{80,48},{96,128},{112,80},... | collective-permute-start | bytes 589832 | tf_op jit(solution)/shard_map/ppermute | solution.py:230
  84.7 13.9 %collective-permute-start.36 = (bf16[128,1536]{1,0:T(8,128)(2,1)S(1)}, bf16[128,1536]{1,0:T(8,128)(2,1)S(1)}, u32[]{:S(2)}, u32[]{:S(2)}) collective-permute-start(bf16[128,1536]{1,0:T(8,128)(2,1)S(1)} %stack.17), channel_id=1, source_target_pairs={{0,16},{16,0},{32,48},{48,32},{64,80},{80,64},{96,112},{112,96},{1... | collective-permute-start | bytes 1179656 | tf_op jit(solution)/shard_map/ppermute | solution.py:224
  85.0 5.6 %collective-permute-start.6 = (bf16[64,1536]{1,0:T(8,128)(2,1)S(1)}, bf16[64,1536]{1,0:T(8,128)(2,1)S(1)}, u32[]{:S(2)}, u32[]{:S(2)}) collective-permute-start(bf16[64,1536]{1,0:T(8,128)(2,1)S(1)} %collective-permute-done.5.second.refs_3_), channel_id=1, source_target_pairs={{0,32},{16,240},{32,64},{48,16},{64,96},{80,48},{96,128},{112,80},... | collective-permute-start | bytes 589832 | tf_op jit(solution)/shard_map/ppermute | solution.py:230
  87.9 5.7 %collective-permute-start.31 = (bf16[64,1536]{1,0:T(8,128)(2,1)S(1)}, bf16[64,1536]{1,0:T(8,128)(2,1)S(1)}, u32[]{:S(2)}, u32[]{:S(2)}) collective-permute-start(bf16[64,1536]{1,0:T(8,128)(2,1)S(1)} %collective-permute-done.30.second.refs_1_), channel_id=1, source_target_pairs={{0,32},{16,240},{32,64},{48,16},{64,96},{80,48},{96,128},{112,80},... | collective-permute-start | bytes 589832 | tf_op jit(solution)/shard_map/ppermute | solution.py:230
  88.0 8.6 %collective-permute-start.24 = (bf16[64,1536]{1,0:T(8,128)(2,1)S(1)}, bf16[64,1536]{1,0:T(8,128)(2,1)S(1)}, u32[]{:S(2)}, u32[]{:S(2)}) collective-permute-start(bf16[64,1536]{1,0:T(8,128)(2,1)S(1)} %collective-permute-done.23.first.refs_0_), channel_id=1, source_target_pairs={{0,32},{16,240},{32,64},{48,16},{64,96},{80,48},{96,128},{112,80},... | collective-permute-start | bytes 589832 | tf_op jit(solution)/shard_map/ppermute | solution.py:230
  90.5 8.2 %collective-permute-start.16 = (bf16[64,1536]{1,0:T(8,128)(2,1)S(1)}, bf16[64,1536]{1,0:T(8,128)(2,1)S(1)}, u32[]{:S(2)}, u32[]{:S(2)}) collective-permute-start(bf16[64,1536]{1,0:T(8,128)(2,1)S(1)} %collective-permute-done.15.first.refs_1_), channel_id=1, source_target_pairs={{0,32},{16,240},{32,64},{48,16},{64,96},{80,48},{96,128},{112,80},... | collective-permute-start | bytes 589832 | tf_op jit(solution)/shard_map/ppermute | solution.py:230
  93.7 7.6 %collective-permute-start.7 = (bf16[64,1536]{1,0:T(8,128)(2,1)S(1)}, bf16[64,1536]{1,0:T(8,128)(2,1)S(1)}, u32[]{:S(2)}, u32[]{:S(2)}) collective-permute-start(bf16[64,1536]{1,0:T(8,128)(2,1)S(1)} %collective-permute-done.6.second.refs_2_), channel_id=1, source_target_pairs={{0,32},{16,240},{32,64},{48,16},{64,96},{80,48},{96,128},{112,80},... | collective-permute-start | bytes 589832 | tf_op jit(solution)/shard_map/ppermute | solution.py:230
  95.8 17.1 %collective-permute-start.33 = (bf16[128,1536]{1,0:T(8,128)(2,1)S(1)}, bf16[128,1536]{1,0:T(8,128)(2,1)S(1)}, u32[]{:S(2)}, u32[]{:S(2)}) collective-permute-start(bf16[128,1536]{1,0:T(8,128)(2,1)S(1)} %stack.14), channel_id=1, source_target_pairs={{0,16},{16,0},{32,48},{48,32},{64,80},{80,64},{96,112},{112,96},{1... | collective-permute-start | bytes 1179656 | tf_op jit(solution)/shard_map/ppermute | solution.py:224
  96.7 16.3 %collective-permute-start.34 = (bf16[128,1536]{1,0:T(8,128)(2,1)S(1)}, bf16[128,1536]{1,0:T(8,128)(2,1)S(1)}, u32[]{:S(2)}, u32[]{:S(2)}) collective-permute-start(bf16[128,1536]{1,0:T(8,128)(2,1)S(1)} %stack.15), channel_id=1, source_target_pairs={{0,16},{16,0},{32,48},{48,32},{64,80},{80,64},{96,112},{112,96},{1... | collective-permute-start | bytes 1179656 | tf_op jit(solution)/shard_map/ppermute | solution.py:224
  98.6 15.6 %collective-permute-start.32 = (bf16[128,1536]{1,0:T(8,128)(2,1)S(1)}, bf16[128,1536]{1,0:T(8,128)(2,1)S(1)}, u32[]{:S(2)}, u32[]{:S(2)}) collective-permute-start(bf16[128,1536]{1,0:T(8,128)(2,1)S(1)} %stack.13), channel_id=1, source_target_pairs={{0,16},{16,0},{32,48},{48,32},{64,80},{80,64},{96,112},{112,96},{1... | collective-permute-start | bytes 1179656 | tf_op jit(solution)/shard_map/ppermute | solution.py:224
  98.7 16.4 %collective-permute-start.17 = (bf16[64,1536]{1,0:T(8,128)(2,1)S(1)}, bf16[64,1536]{1,0:T(8,128)(2,1)S(1)}, u32[]{:S(2)}, u32[]{:S(2)}) collective-permute-start(bf16[64,1536]{1,0:T(8,128)(2,1)S(1)} %collective-permute-done.16.refs_1_), channel_id=1, source_target_pairs={{0,16},{16,0},{32,48},{48,32},{64,80},{80,64},{96,112},{112,96},{1... | collective-permute-start | bytes 589832 | tf_op jit(solution)/shard_map/ppermute | solution.py:224
  101.3 14.7 %collective-permute-start.8 = (bf16[64,1536]{1,0:T(8,128)(2,1)S(1)}, bf16[64,1536]{1,0:T(8,128)(2,1)S(1)}, u32[]{:S(2)}, u32[]{:S(2)}) collective-permute-start(bf16[64,1536]{1,0:T(8,128)(2,1)S(1)} %collective-permute-done.7.refs_1_), channel_id=1, source_target_pairs={{0,16},{16,0},{32,48},{48,32},{64,80},{80,64},{96,112},{112,96},{1... | collective-permute-start | bytes 589832 | tf_op jit(solution)/shard_map/ppermute | solution.py:224
